TPU v7x, 32 devices: a whole 2x2x4 slice. The times are simulated.
32 devices in a mesh: dp: 16 (over z, y, x), seq: 2 (over core).
Axes of the slice: x: 2, y: 2, z: 4, core: 2. Of those that a mesh axis runs over, the one named last changes fastest.
Arguments:
- patches: bfloat16 [32, 256, 768], P('dp', 'seq'), may hold values from -6 to 6
- block_masks: int32 [32, 196], P('dp'), may hold values from 0 to 1, as said below
- split_rows: int32 [32], P('dp'), may hold values from 6 to 8, as said below
- span_order: int32 [2720], replicated, may hold values from 0 to 2719, as said below
- weights: float32 [10880, 768], P('dp')
- teacher: bfloat16 [10880, 768], P('dp')
- first_moment: float32 [10880, 768], P('dp')
- second_moment: float32 [10880, 768], P('dp')
- step_count: int32 [1], replicated, may hold values from 2 to 20
Outputs:
- total_loss: float32 [], replicated
- grad_norm: float32 [], replicated
- updated_weights: float32 [10880, 768], P('dp')
- weights_copy: bfloat16 [10880, 768], P('dp')
- updated_first: float32 [10880, 768], P('dp')
- updated_second: float32 [10880, 768], P('dp')
Inputs may be any that keep to these rules, and one draw needn't show every extreme that they name: `block_masks`: cells are row-major over the 14 x 14 grid; masks come in aligned 2 x 2 blocks of cells. Rows 0 to split_rows - 1 of an image lie on seq index 0 after its CLS slot, the rest on seq index 1 from slot 0. `span_order`: each of 0 to 2719 once.
All inputs are finite; a program needn't handle non-finite values.
Results may differ from a plain program's by a relative error of at most 0.001.
The roundings to bfloat16 on the way count: a program that leaves them out, or rounds other values in their place, can miss the bound.
Values may be sent and summed in bfloat16 or wider, within the bound.
A program may use at most 256 MiB of HBM per device.

v0:
```python
import math

import jax
import jax.numpy as jnp
from jax import lax
from jax.sharding import PartitionSpec as P

D = 768
HEADS = 12
HD = 64
FF = 3072
PP = 768
GRID = 14
SL = 128
CR = 4


BETA = 2.0
CLIP = 0.01
LEARN = 0.03
DECAY = 0.05
BETA_ONE = 0.9
BETA_TWO = 0.999
ADAM_EPS = 1e-08
NORM_EPS = 1e-06


def from_partner(shard, axis, bit):
    return lax.ppermute(shard, axis, [(i, i ^ 1 << bit) for i in range(lax.axis_size(axis))])


def layout():
    return [
        ("cls", 1, (D,)),
        ("mask_tok", 1, (D,)),
        ("b_pe", 1, (D,)),
        ("ln1_g", 1, (D,)),
        ("ln1_b", 1, (D,)),
        ("b_out", 1, (D,)),
        ("ln2_g", 1, (D,)),
        ("ln2_b", 1, (D,)),
        ("b_two", 1, (D,)),
        ("lnf_g", 1, (D,)),
        ("lnf_b", 1, (D,)),
        ("b_head", 1, (D,)),
        ("b_one", FF // D, (FF,)),
        ("w_pe", PP, (PP, D)),
        ("w_qkv", 3 * D, (D, 3 * D)),
        ("w_out", D, (D, D)),
        ("w_one", FF, (D, FF)),
        ("w_two", FF, (FF, D)),
        ("w_head", D, (D, D)),
    ]


def unpack(flat):
    tables = {}
    offset = 0
    for entry_name, entry_rows, entry_shape in layout():
        tables[entry_name] = flat[offset : offset + entry_rows].reshape(entry_shape)
        offset = offset + entry_rows
    return tables


def pack_flat(tables, total_rows):
    pieces = [tables[entry_name].reshape(-1, D) for entry_name, entry_rows, entry_shape in layout()]
    stacked = jnp.concatenate(pieces, 0)
    return jnp.concatenate(
        [stacked, jnp.zeros((total_rows - stacked.shape[0], D), stacked.dtype)], 0
    )


def reorder(stored, order):
    return stored.reshape(order.shape[0], -1, D)[order].reshape(-1, D)


def slot_info(split_rows, seq_side):
    column = jnp.arange(SL)[None, :]
    split_col = split_rows[:, None]
    first_side = seq_side == 0
    first_slot = jnp.where(first_side, 1, 0)
    filled = jnp.where(first_side, split_col * GRID, (GRID - split_col) * GRID)
    offset = jnp.where(first_side, -1, split_col * GRID)
    is_patch = (column >= first_slot) & (column < first_slot + filled)
    is_cls = first_side & (column == 0) & (split_col >= 0)
    grid_cell = jnp.clip(column + offset, 0, GRID * GRID - 1)
    return (is_patch, is_cls, grid_cell)


def sincos(grid_cell):
    quarter = D // 4
    frequency = 1.0 / 10000.0 ** (jnp.arange(quarter).astype(jnp.float32) / quarter)
    rows_at = (grid_cell // GRID).astype(jnp.float32)[..., None] * frequency
    cols_at = (grid_cell % GRID).astype(jnp.float32)[..., None] * frequency
    return jnp.concatenate(
        [jnp.sin(rows_at), jnp.cos(rows_at), jnp.sin(cols_at), jnp.cos(cols_at)], -1
    )


def layer_norm(values):
    center = jnp.mean(values, -1, keepdims=True)
    centred = values - center
    return centred * lax.rsqrt(jnp.mean(centred * centred, -1, keepdims=True) + NORM_EPS)


def matmul_f32(left_mat, right_mat):
    return jnp.dot(left_mat, right_mat, preferred_element_type=jnp.float32)


def weight_grad(left_mat, right_mat):
    return lax.dot_general(
        left_mat, right_mat, (((0,), (0,)), ((), ())), preferred_element_type=jnp.float32
    )


def back_dot(left_mat, right_mat):
    return lax.dot_general(
        left_mat, right_mat, (((1,), (1,)), ((), ())), preferred_element_type=jnp.float32
    )


def vector(params, entry_name):
    return params[entry_name].astype(jnp.float32)


def column_sums(values):
    return jnp.sum(values.astype(jnp.float32), 0)


def norm_fwd(values, gain_vec, bias_vec):
    center = jnp.mean(values, -1, keepdims=True)
    centred = values - center
    inverse = lax.rsqrt(jnp.mean(centred * centred, -1, keepdims=True) + NORM_EPS)
    normed = centred * inverse
    return (normed * gain_vec + bias_vec, normed, inverse)


def norm_back(grad_out, normed, inverse, gain_vec):
    scaled = grad_out * gain_vec
    grad_in = inverse * (
        scaled
        - jnp.mean(scaled, -1, keepdims=True)
        - normed * jnp.mean(scaled * normed, -1, keepdims=True)
    )
    return (grad_in, jnp.sum(grad_out * normed, 0), jnp.sum(grad_out, 0))


def place_tokens(params, embedded, is_patch, is_cls, hidden_mask, position):
    on_grid = embedded.reshape(is_patch.shape + (D,)) + position
    tokens = jnp.where(is_patch[..., None], on_grid, 0.0)
    tokens = jnp.where(hidden_mask[..., None], vector(params, "mask_tok") + position, tokens)
    tokens = jnp.where(is_cls[..., None], vector(params, "cls"), tokens)
    return tokens.reshape(-1, D)


def project(params, tokens, length):
    normed_in, normed, inverse = norm_fwd(tokens, vector(params, "ln1_g"), vector(params, "ln1_b"))
    normed_in = normed_in.astype(jnp.bfloat16)
    packed = (
        matmul_f32(normed_in, params["w_qkv"])
        .astype(jnp.bfloat16)
        .reshape(-1, length, 3, HEADS, HD)
    )
    return (normed_in, normed, inverse, packed[:, :, 0], packed[:, :, 1], packed[:, :, 2])


def scores_of(queries, keys_block, key_live):
    raw_scores = jnp.einsum(
        "bqhd,bkhd->bhqk", queries, keys_block, preferred_element_type=jnp.float32
    ) * HD ** (-0.5)
    return jnp.where(key_live[:, None, None, :], raw_scores, -1e30)


def attend(queries, blocks):
    scores = [scores_of(queries, block[0], block[2]) for block in blocks]
    highest = reduce_max([jnp.max(member, -1, keepdims=True) for member in scores])
    summed = sum([jnp.sum(jnp.exp(member - highest), -1, keepdims=True) for member in scores])
    logsum = highest + jnp.log(summed)
    mixed_out = sum(
        [
            jnp.einsum(
                "bhqk,bkhd->bqhd",
                jnp.exp(member - logsum).astype(jnp.bfloat16),
                block[1],
                preferred_element_type=jnp.float32,
            )
            for member, block in zip(scores, blocks)
        ]
    )
    return (mixed_out.astype(jnp.bfloat16).reshape(-1, D), logsum)


def reduce_max(members):
    highest = members[0]
    for member in members[1:]:
        highest = jnp.maximum(highest, member)
    return highest


def finish(params, tokens, queries, blocks):
    mixed_out, logsum = attend(queries, blocks)
    hidden = tokens + matmul_f32(mixed_out, params["w_out"]) + vector(params, "b_out")
    normed_two_in, normed_two, inverse_two = norm_fwd(
        hidden, vector(params, "ln2_g"), vector(params, "ln2_b")
    )
    normed_two_in = normed_two_in.astype(jnp.bfloat16)
    upward = matmul_f32(normed_two_in, params["w_one"]) + vector(params, "b_one")
    gelled = jax.nn.gelu(upward).astype(jnp.bfloat16)
    output = hidden + matmul_f32(gelled, params["w_two"]) + vector(params, "b_two")
    return (output, (mixed_out, logsum, normed_two, inverse_two, normed_two_in, upward, gelled))


def layer_back(params, grad_out, saved, far_blocks, key_live, gradients):
    (
        normed_in,
        normed,
        inverse,
        queries,
        keys_loc,
        values_loc,
        mixed_out,
        logsum,
        normed_two,
        inverse_two,
        normed_two_in,
        upward,
        gelled,
    ) = saved
    length = queries.shape[1]
    blocks = [(keys_loc, values_loc, key_live)] + far_blocks
    grad_branch = grad_out.astype(jnp.bfloat16)
    gradients["w_two"] = weight_grad(gelled, grad_branch)
    gradients["b_two"] = column_sums(grad_branch)
    unused, gelu_pull = jax.vjp(jax.nn.gelu, upward)
    grad_up = gelu_pull(back_dot(grad_branch, params["w_two"]))[0].astype(jnp.bfloat16)
    gradients["w_one"] = weight_grad(normed_two_in, grad_up)
    gradients["b_one"] = column_sums(grad_up)
    grad_two, gradients["ln2_g"], gradients["ln2_b"] = norm_back(
        back_dot(grad_up, params["w_one"]), normed_two, inverse_two, vector(params, "ln2_g")
    )
    grad_hidden = grad_out + grad_two
    grad_attn = grad_hidden.astype(jnp.bfloat16)
    gradients["w_out"] = weight_grad(mixed_out, grad_attn)
    gradients["b_out"] = column_sums(grad_attn)
    grad_mixed = (
        back_dot(grad_attn, params["w_out"]).astype(jnp.bfloat16).reshape(-1, length, HEADS, HD)
    )
    probs = [jnp.exp(scores_of(queries, block[0], block[2]) - logsum) for block in blocks]
    pushes = [
        jnp.einsum("bqhd,bkhd->bhqk", grad_mixed, block[1], preferred_element_type=jnp.float32)
        for block in blocks
    ]
    common = sum([jnp.sum(prob * push, -1, keepdims=True) for prob, push in zip(probs, pushes)])
    grad_scores = [
        (prob * (push - common)).astype(jnp.bfloat16) for prob, push in zip(probs, pushes)
    ]
    key_scale = HD ** (-0.5)
    grad_queries = (
        sum(
            [
                jnp.einsum("bhqk,bkhd->bqhd", member, block[0], preferred_element_type=jnp.float32)
                for member, block in zip(grad_scores, blocks)
            ]
        )
        * key_scale
    )
    key_grads = [
        jnp.einsum("bhqk,bqhd->bkhd", member, queries, preferred_element_type=jnp.float32)
        * key_scale
        for member in grad_scores
    ]
    value_grads = [
        jnp.einsum(
            "bhqk,bqhd->bkhd",
            prob.astype(jnp.bfloat16),
            grad_mixed,
            preferred_element_type=jnp.float32,
        )
        for prob in probs
    ]
    grad_keys, grad_values = (key_grads[0], value_grads[0])
    returned = from_partner(
        jnp.stack([key_grads[1], value_grads[1]]).astype(jnp.bfloat16), "seq", 0
    ).astype(jnp.float32)
    grad_keys = grad_keys + returned[0]
    grad_values = grad_values + returned[1]
    grad_packed = (
        jnp.stack([grad_queries, grad_keys, grad_values], 2).astype(jnp.bfloat16).reshape(-1, 3 * D)
    )
    gradients["w_qkv"] = weight_grad(normed_in, grad_packed)
    grad_first, gradients["ln1_g"], gradients["ln1_b"] = norm_back(
        back_dot(grad_packed, params["w_qkv"]), normed, inverse, vector(params, "ln1_g")
    )
    return grad_hidden + grad_first


def on_device(
    patches,
    block_masks,
    split_rows,
    span_order,
    weights,
    teacher,
    first_moment,
    second_moment,
    step_count,
):
    gathered, teacher_all = (
        lax.all_gather(weights.astype(jnp.bfloat16), "dp", axis=0, tiled=True),
        lax.all_gather(teacher, "dp", axis=0, tiled=True),
    )
    inverse_order = jnp.argsort(span_order)
    params = unpack(reorder(gathered, inverse_order))
    teacher_params = unpack(reorder(teacher_all, inverse_order))
    seq_side = lax.axis_index("seq")
    is_patch, is_cls, grid_cell = slot_info(split_rows, seq_side)
    far_patch, far_cls, far_cell = slot_info(split_rows, 1 - seq_side)
    far_live = far_patch | far_cls
    length = SL
    images = patches.shape[0]
    hidden_mask = (jnp.take_along_axis(block_masks, grid_cell, 1) == 1) & is_patch
    key_live = is_patch | is_cls
    masked_count = lax.psum(jnp.sum(hidden_mask.astype(jnp.float32)), ("dp", "seq"))
    position = sincos(grid_cell)
    pixels = patches.reshape(-1, PP)
    embedded_teacher = matmul_f32(pixels, teacher_params["w_pe"]) + vector(teacher_params, "b_pe")
    embedded_student = matmul_f32(pixels, params["w_pe"]) + vector(params, "b_pe")
    tokens_teacher = place_tokens(
        teacher_params, embedded_teacher, is_patch, is_cls, jnp.zeros_like(hidden_mask), position
    )
    tokens_student = place_tokens(params, embedded_student, is_patch, is_cls, hidden_mask, position)
    teacher_proj = project(teacher_params, tokens_teacher, length)
    student_proj = project(params, tokens_student, length)
    arrived = from_partner(
        jnp.stack([teacher_proj[4], teacher_proj[5], student_proj[4], student_proj[5]]), "seq", 0
    )
    teacher_far = [(arrived[0], arrived[1], far_live)]
    student_far = [(arrived[2], arrived[3], far_live)]
    teacher_out, unused = finish(
        teacher_params,
        tokens_teacher,
        teacher_proj[3],
        [(teacher_proj[4], teacher_proj[5], key_live)] + teacher_far,
    )
    target = layer_norm(teacher_out)
    student_out, finish_saved = finish(
        params,
        tokens_student,
        student_proj[3],
        [(student_proj[4], student_proj[5], key_live)] + student_far,
    )
    final_in, final_normed, final_inverse = norm_fwd(
        student_out, vector(params, "lnf_g"), vector(params, "lnf_b")
    )
    final_in = final_in.astype(jnp.bfloat16)
    predicted = matmul_f32(final_in, params["w_head"]) + vector(params, "b_head")
    difference = predicted - target
    magnitude = jnp.abs(difference)
    elementwise = jnp.where(
        magnitude < BETA, 0.5 * difference * difference / BETA, magnitude - 0.5 * BETA
    )
    selected = hidden_mask.reshape(-1)[:, None]
    loss_scale = 1.0 / (math.sqrt(D) * masked_count)
    total_loss = lax.psum(
        jnp.sum(jnp.where(selected, elementwise, 0.0)) * loss_scale, ("dp", "seq")
    )
    grad_pred = (
        jnp.where(selected, jnp.clip(difference / BETA, -1.0, 1.0), 0.0) * loss_scale
    ).astype(jnp.bfloat16)
    gradients = {}
    gradients["w_head"] = weight_grad(final_in, grad_pred)
    gradients["b_head"] = column_sums(grad_pred)
    grad_tokens, gradients["lnf_g"], gradients["lnf_b"] = norm_back(
        back_dot(grad_pred, params["w_head"]), final_normed, final_inverse, vector(params, "lnf_g")
    )
    saved = tuple(student_proj) + tuple(finish_saved)
    grad_tokens = layer_back(params, grad_tokens, saved, student_far, key_live, gradients)
    grad_slots = grad_tokens.reshape(images, length, D)
    visible = (is_patch & jnp.logical_not(hidden_mask))[..., None]
    grad_embed = jnp.where(visible, grad_slots, 0.0).astype(jnp.bfloat16).reshape(-1, D)
    gradients["w_pe"] = weight_grad(pixels, grad_embed)
    gradients["b_pe"] = column_sums(grad_embed)
    gradients["mask_tok"] = jnp.sum(jnp.where(hidden_mask[..., None], grad_slots, 0.0), (0, 1))
    gradients["cls"] = jnp.sum(jnp.where(is_cls[..., None], grad_slots, 0.0), (0, 1))
    stored_grad = reorder(pack_flat(gradients, span_order.shape[0] * CR), span_order)
    owned_grad = lax.psum_scatter(stored_grad, "dp", scatter_dimension=0, tiled=True)
    owned_grad = lax.psum(owned_grad, "seq")
    squares = lax.psum(jnp.sum(owned_grad * owned_grad), "dp")
    grad_norm = jnp.sqrt(squares)
    clipped = owned_grad * (CLIP / jnp.maximum(grad_norm, CLIP))
    updated_first = BETA_ONE * first_moment + (1.0 - BETA_ONE) * clipped
    updated_second = BETA_TWO * second_moment + (1.0 - BETA_TWO) * clipped * clipped
    steps_done = step_count[0].astype(jnp.float32)
    adam_step = (
        updated_first
        / (1.0 - BETA_ONE**steps_done)
        / (jnp.sqrt(updated_second / (1.0 - BETA_TWO**steps_done)) + ADAM_EPS)
    )
    updated_weights = weights - LEARN * (adam_step + DECAY * weights)
    return (
        total_loss,
        grad_norm,
        updated_weights,
        updated_weights.astype(jnp.bfloat16),
        updated_first,
        updated_second,
    )


def solution(mesh):
    placed = (
        P("dp", "seq", None),
        P("dp", None),
        P("dp"),
        P(),
        P("dp", None),
        P("dp", None),
        P("dp", None),
        P("dp", None),
        P(),
    )
    return jax.shard_map(
        on_device,
        mesh=mesh,
        in_specs=placed,
        out_specs=(P(), P(), P("dp", None), P("dp", None), P("dp", None), P("dp", None)),
        check_vma=False,
    )
```

profile of v0, /device:TPU:0, one launch (start us, length us, event | category | flops | bytes accessed | tf_op | source)
XLA Modules:
  0.0 1527.8 jit_solution(8221068962807406303)
XLA Ops:
  8.0 2.7 convert_element_type.232
  14.6 44.4 %psum.28 = f32[]{:T(128)} all-reduce(f32[]{:T(128)} %convert_reduce_fusion.5), channel_id=1, replica_groups=mesh['dp'=16,'seq'=2] {'dp','seq'}, use_global_device_ids=true, to_apply=%region_23.24 | all-reduce | flops 1 | bytes 8 | tf_op jit(solution)/shard_map/psum | solution.py:323
  59.7 5.8 sort.17
  67.6 2.7 multiply_sine_fusion.1
  70.2 135.1 %all-gather.5.cloned.1.call-done = bf16[10880,768]{1,0:T(8,128)(2,1)} async-done(((bf16[680,768]{1,0:T(8,128)(2,1)}), bf16[10880,768]{1,0:T(8,128)(2,1)}) %all-gather.5.cloned.1.call-update) | async-done | bytes 16711696 | tf_op jit(solution)/shard_map/all_gather | solution.py:310
  205.3 28.0 %reshape.817 = bf16[2720,4,768]{2,1,0:T(4,128)(2,1)} reshape(bf16[10880,768]{1,0:T(8,128)(2,1)} %all-gather.5.cloned.1.call-done) | data formatting | bytes 33423360 | tf_op jit(solution)/shard_map/reshape | solution.py:74
  233.4 26.2 %gather_fusion.1 = bf16[2720,4,768]{2,1,0:T(4,128)(2,1)} fusion(bf16[2720,4,768]{2,1,0:T(4,128)(2,1)} %reshape.817, s32[3072]{0:T(1024)S(1)} %pad_clamp_fusion.1), kind=kCustom, calls=%fused_computation.1 | custom fusion | bytes 33434240 | tf_op jit(solution)/shard_map/gather | solution.py:74
  259.6 26.7 %reshape.818 = bf16[10880,768]{1,0:T(8,128)(2,1)} reshape(bf16[2720,4,768]{2,1,0:T(4,128)(2,1)} %gather_fusion.1) | data formatting | bytes 33423360 | tf_op jit(solution)/shard_map/reshape | solution.py:74
  286.3 5.0 slice.238
  291.3 3.8 fusion.164
  295.2 102.2 %all-gather.3.cloned.1.call-done = bf16[10880,768]{1,0:T(8,128)(2,1)} async-done(((bf16[680,768]{1,0:T(8,128)(2,1)}), bf16[10880,768]{1,0:T(8,128)(2,1)}) %all-gather.3.cloned.1.call-update) | async-done | bytes 16711696 | tf_op jit(solution)/shard_map/all_gather | solution.py:309
  397.3 27.9 %reshape.812 = bf16[2720,4,768]{2,1,0:T(4,128)(2,1)} reshape(bf16[10880,768]{1,0:T(8,128)(2,1)} %all-gather.3.cloned.1.call-done) | data formatting | bytes 33423360 | tf_op jit(solution)/shard_map/reshape | solution.py:74
  425.2 26.4 %gather_fusion = bf16[2720,4,768]{2,1,0:T(4,128)(2,1)} fusion(bf16[2720,4,768]{2,1,0:T(4,128)(2,1)} %reshape.812, s32[3072]{0:T(1024)S(1)} %pad_clamp_fusion.1), kind=kCustom, calls=%fused_computation | custom fusion | bytes 33434240 | tf_op jit(solution)/shard_map/gather | solution.py:74
  451.6 5.0 slice.229
  456.7 26.6 %reshape.813 = bf16[10880,768]{1,0:T(8,128)(2,1)} reshape(bf16[2720,4,768]{2,1,0:T(4,128)(2,1)} %gather_fusion) | data formatting | bytes 33423360 | tf_op jit(solution)/shard_map/reshape | solution.py:74
  483.3 4.3 fusion.162
  487.6 10.6 fusion.163
  501.1 3.2 slice.176
  504.3 3.2 slice.204
  507.4 17.8 %reshape.819 = bf16[768,2304]{1,0:T(8,128)(2,1)} reshape(bf16[576,4,768]{2,1,0:T(4,128)(2,1)} %slice.238) | data formatting | bytes 7077888 | tf_op jit(solution)/shard_map/reshape | solution.py:60
  532.8 3.5 reshape.820
  536.4 3.3 fusion.166
  539.6 7.2 reshape.815
  548.6 3.2 slice.166
  559.4 3.5 reshape.816
  567.6 8.5 slice.211
  576.1 5.5 copy.83
  584.5 10.5 fusion.161
  595.1 9.0 slice.193
  604.1 5.6 copy.81
  619.0 7.5 fusion.172
  633.5 4.7 convolution_add_fusion.1
  644.5 3.8 convert_reduce_fusion
  661.6 5.2 fusion.156
  679.1 11.8 reshape.841
  692.3 7.7 fusion.145
  707.0 4.2 fusion.42
  711.9 8.4 reshape.840
  722.5 78.6 %concatenate.9 = f32[10880,768]{1,0:T(8,128)} concatenate(f32[1,768]{1,0:T(1,128)S(1)} %reshape.826, f32[1,768]{1,0:T(1,128)S(1)} %reshape.827, f32[1,768]{1,0:T(1,128)S(1)} %reshape.828, f32[1,768]{1,0:T(1,128)S(1)} %reshape.829, f32[1,768]{1,0:T(1,128)S(1)} %reshape.830, f32[1,768]{1,0:T(1,128)S(1)} %copy-done.82, f32[1,768]{1,0:T(1,128)S(1)} %copy-done.83, ...), dimensions={0} | concatenate | bytes 66846720 | tf_op jit(solution)/shard_map/concatenate | solution.py:68
  801.1 37.8 %reshape.842 = f32[2720,4,768]{2,1,0:T(4,128)} reshape(f32[10880,768]{1,0:T(8,128)} %concatenate.9) | data formatting | bytes 66846720 | tf_op jit(solution)/shard_map/reshape | solution.py:74
  838.9 32.5 %gather_fusion.2 = f32[2720,4,768]{2,1,0:T(4,128)} fusion(f32[2720,4,768]{2,1,0:T(4,128)} %reshape.842, s32[3072]{0:T(1024)S(1)} %copy-done.60), kind=kCustom, calls=%fused_computation.2 | custom fusion | bytes 66857600 | tf_op jit(solution)/shard_map/gather | solution.py:74
  871.4 38.5 %reshape.843 = f32[10880,768]{1,0:T(8,128)} reshape(f32[2720,4,768]{2,1,0:T(4,128)} %gather_fusion.2) | data formatting | bytes 66846720 | tf_op jit(solution)/shard_map/reshape | solution.py:74
  910.0 494.6 %reduce-scatter.2.cloned.1.call-done = f32[680,768]{1,0:T(8,128)} async-done(((f32[10880,768]{1,0:T(8,128)}), f32[680,768]{1,0:T(8,128)}) %reduce-scatter.2.cloned.1.call-update) | async-done | bytes 2088976 | tf_op jit(solution)/shard_map/reduce_scatter | solution.py:386
  1406.2 21.3 %all-reduce.2.cloned.1.call-done = f32[680,768]{1,0:T(8,128)} async-done(((f32[680,768]{1,0:T(8,128)}), f32[680,768]{1,0:T(8,128)}) %all-reduce.2.cloned.1.call-update) | async-done | bytes 2088976 | tf_op jit(solution)/shard_map/psum | solution.py:387
  1427.5 2.7 multiply_reduce_fusion
  1430.3 40.5 %psum.29 = f32[]{:T(128)} all-reduce(f32[]{:T(128)S(6)} %mul.479), channel_id=1, replica_groups=mesh['dp'=16,'seq'=2] {'dp','seq'}, use_global_device_ids=true, to_apply=%region_24.25 | all-reduce | flops 1 | bytes 8 | tf_op jit(solution)/shard_map/psum | solution.py:364
  1470.7 41.3 %psum.31 = f32[]{:T(128)} all-reduce(f32[]{:T(128)} %multiply_reduce_fusion), channel_id=1, replica_groups=mesh['dp'=16,'seq'=2] {'dp'}, use_global_device_ids=true, to_apply=%region_49.50 | all-reduce | flops 1 | bytes 8 | tf_op jit(solution)/shard_map/psum | solution.py:388
  1512.8 6.9 fusion.158
  (363 shorter events, 92.2 us)
Async XLA Ops:
  7.2 518.1 %copy-start = (bf16[2,128,768]{2,1,0:T(8,128)(2,1)S(1)}, bf16[2,128,768]{2,1,0:T(8,128)(2,1)}, u32[]{:S(2)}) copy-start(bf16[2,128,768]{2,1,0:T(8,128)(2,1)} %param.9) | copy-start | bytes 1179652
  7.2 198.1 %all-gather.5.cloned.1.call-start = ((), (), s32[]{:S(2)}) async-start(), calls=%async_computation.2 | async-start | bytes 17756160 | tf_op jit(solution)/shard_map/all_gather | solution.py:310
  7.9 51.8 %copy-start.61 = (s32[2720]{0:T(1024)S(1)}, s32[2720]{0:T(1024)}, u32[]{:S(2)}) copy-start(s32[2720]{0:T(1024)} %param.12) | copy-start | bytes 32644
  7.9 389.4 %all-gather.3.cloned.1.call-start = ((), (), s32[]{:S(2)}) async-start(), calls=%async_computation.1 | async-start | bytes 17756160 | tf_op jit(solution)/shard_map/all_gather | solution.py:309
  10.7 1394.0 %reduce-scatter.2.cloned.1.call-start = ((), (), s32[]{:S(2)}) async-start(), calls=%async_computation.3 | async-start | bytes 35512320 | tf_op jit(solution)/shard_map/reduce_scatter | solution.py:386
  548.6 5.6 copy-start.54
  548.6 5.6 copy-start.58
  562.9 3.2 copy-start.42
  565.1 46.4 %copy-start.31 = (bf16[2,128,1,12,64]{1,0,4,3,2:T(2,128)(2,1)}, bf16[2,128,1,12,64]{1,0,4,3,2:T(2,128)(2,1)S(1)}, u32[]{:S(2)}) copy-start(bf16[2,128,1,12,64]{1,0,4,3,2:T(2,128)(2,1)S(1)} %get-tuple-element.74) | copy-start | bytes 1179652
  565.1 46.4 %copy-start.34 = (bf16[2,128,1,12,64]{1,0,4,3,2:T(2,128)(2,1)}, bf16[2,128,1,12,64]{1,0,4,3,2:T(2,128)(2,1)S(1)}, u32[]{:S(2)}) copy-start(bf16[2,128,1,12,64]{1,0,4,3,2:T(2,128)(2,1)S(1)} %get-tuple-element.76) | copy-start | bytes 1179652
  567.6 45.1 %collective-permute-start = (bf16[4,2,128,12,64]{2,4,3,1,0:T(8,128)(2,1)}, bf16[4,2,128,12,64]{2,4,3,1,0:T(8,128)(2,1)}, u32[]{:S(2)}, u32[]{:S(2)}) collective-permute-start(bf16[4,2,128,12,64]{2,4,3,1,0:T(8,128)(2,1)} %pad_maximum_fusion), channel_id=1, source_target_pairs={{0,1},{1,0},{2,3},{3,2},{4,5},{5,4},{6,7},{7,6},{8,9},{9,8},{10,11... | collective-permute-start | bytes 4718600 | tf_op jit(solution)/shard_map/ppermute | solution.py:29
  576.1 5.5 copy-start.62
  604.0 6.9 copy-start.43
  604.0 6.9 copy-start.49
  604.1 6.9 copy-start.106
  632.5 5.7 slice-start.2
  633.1 17.3 %copy-start.8 = (f32[256,768]{1,0:T(8,128)}, f32[256,768]{1,0:T(8,128)S(1)}, u32[]{:S(2)}) copy-start(f32[256,768]{1,0:T(8,128)S(1)} %get-tuple-element.114) | copy-start | bytes 2359300
  633.2 17.2 %copy-start.68 = (f32[256]{0:T(256)}, f32[256]{0:T(256)S(1)}, u32[]{:S(2)}) copy-start(f32[256]{0:T(256)S(1)} %broadcast_multiply_fusion.9) | copy-start | bytes 3076
  633.4 17.0 %copy-start.80 = (f32[256]{0:T(256)}, f32[256]{0:T(256)S(1)}, u32[]{:S(2)}) copy-start(f32[256]{0:T(256)S(1)} %add_rsqrt_fusion.3) | copy-start | bytes 3076
  633.5 4.8 slice-start.3
  633.5 4.8 copy-start.101
  638.2 6.2 copy-start.26
  640.4 3.1 copy-start.17
  640.4 3.1 copy-start.72
  643.5 4.7 slice-start
  644.4 6.0 copy-start.15
  644.4 3.8 slice-start.1
  661.6 5.3 copy-start.18
  661.6 5.3 copy-start.51
  661.6 5.3 copy-start.65
  661.6 5.2 copy-start.73
  661.6 5.2 copy-start.77
  661.6 5.2 copy-start.93
  672.4 3.7 copy-start.74
  672.4 4.2 copy-start.97
  672.4 4.8 copy-start.96
  672.5 5.4 copy-start.95
  672.5 6.0 copy-start.90
  673.4 26.6 %collective-permute-start.1 = (bf16[2,2,128,12,64]{2,4,3,1,0:T(8,128)(2,1)}, bf16[2,2,128,12,64]{2,4,3,1,0:T(8,128)(2,1)}, u32[]{:S(2)}, u32[]{:S(2)}) collective-permute-start(bf16[2,2,128,12,64]{2,4,3,1,0:T(8,128)(2,1)} %pad_maximum_fusion.2), channel_id=1, source_target_pairs={{0,1},{1,0},{2,3},{3,2},{4,5},{5,4},{6,7},{7,6},{8,9},{9,8},{10,11... | collective-permute-start | bytes 2359304 | tf_op jit(solution)/shard_map/ppermute | solution.py:29
  679.1 11.8 copy-start.20
  707.0 4.3 copy-start.7
  707.0 4.3 copy-start.103
  707.0 4.3 copy-start.104
  707.0 4.3 copy-start.109
  711.8 8.5 copy-start.102
  801.1 37.8 %copy-start.60 = (s32[3072]{0:T(1024)S(1)}, s32[3072]{0:T(1024)}, u32[]{:S(2)}) copy-start(s32[3072]{0:T(1024)} %pad_clamp_fusion) | copy-start | bytes 36868
  909.9 517.6 %all-reduce.2.cloned.1.call-start = ((), (), s32[]{:S(2)}) async-start(), calls=%async_computation.4 | async-start | bytes 4177920 | tf_op jit(solution)/shard_map/psum | solution.py:387
  1404.6 108.1 %copy-start.14 = (f32[680,768]{1,0:T(8,128)S(1)}, f32[680,768]{1,0:T(8,128)}, u32[]{:S(2)}) copy-start(f32[680,768]{1,0:T(8,128)} %param.13) | copy-start | bytes 6266884
  (72 other events, 143.9 us)
Sparse Core Ops, SparseCore 0:
  10.8 194.4 all-gather.4
  208.7 188.5 all-gather.2
  910.1 494.5 reduce-scatter.1
  1406.8 20.6 all-reduce.1
where the time goes:
time: 1550 us; the launch traced here: 1530 us
  waiting for transfers between devices  754 us (49%)
  local copies, waits for them, and re-layouts  512 us (33%)
  blocking collectives  126 us (8%)
  matrix products  74.8 us (5%)
  other arithmetic  40.3 us (3%)
  between operations  19.9 us (1%)
    reduce_scatter x1, waiting for transfers between devices, on_device(): lax.psum_scatter(stored_grad, 'dp', scatter_dimension=0, tiled=True)  495 us
    reshape x6, local copies, waits for them, and re-layouts, reorder(): return stored.reshape(order.shape[0], -1, D)[order].reshape(-1, D)  186 us
    all_gather x1, waiting for transfers between devices, on_device(): lax.all_gather(teacher, 'dp', axis=0, tiled=True)  135 us
    all_gather x1, waiting for transfers between devices, on_device(): lax.all_gather(weights.astype(jnp.bfloat16), 'dp', axis=0, tiled=True)  102 us
    gather x3, local copies, waits for them, and re-layouts, reorder(): return stored.reshape(order.shape[0], -1, D)[order].reshape(-1, D)  85.2 us
    concatenate x1, local copies, waits for them, and re-layouts, pack_flat(): jnp.concatenate([stacked, jnp.zeros((total_rows - stacked.shape[0], D), s...  78.6 us
    slice x13, local copies, waits for them, and re-layouts, unpack(): tables[entry_name] = flat[offset:offset + entry_rows].reshape(entry_shape)  68.6 us
    psum x1, blocking collectives, on_device(): lax.psum(jnp.sum(hidden_mask.astype(jnp.float32)), ('dp', 'seq'))  44.4 us
  transfers between devices with their start and end apart: 6, of which 4 were waited for; matrix products, arithmetic and copies ran while one was open for 12% of the time, Pallas kernels for 0%

commit v1 on v0

--- a/solution.py
+++ b/solution.py
@@ -1,8 +1,11 @@
+import functools
 import math
 
 import jax
 import jax.numpy as jnp
 from jax import lax
+from jax.experimental import pallas as pl
+from jax.experimental.pallas import tpu as pltpu
 from jax.sharding import PartitionSpec as P
 
 D = 768
@@ -27,6 +30,477 @@
 
 def from_partner(shard, axis, bit):
     return lax.ppermute(shard, axis, [(i, i ^ 1 << bit) for i in range(lax.axis_size(axis))])
+
+
+MESH = pl.DeviceIdType.MESH
+ZN = 4
+
+
+def place():
+    p = lax.axis_index("dp")
+    return p, p // 4, (p // 2) % 2, p % 2, lax.axis_index("seq")
+
+
+def to_chip(p, s):
+    return (p, s)
+
+
+def greet(p, z, s):
+    barrier = pltpu.get_barrier_semaphore()
+
+    def hello(dev):
+        pl.semaphore_signal(barrier, inc=1, device_id=dev, device_id_type=MESH)
+
+    hello((p, 1 - s))
+    hello((p ^ 1, s))
+    hello((p ^ 2, s))
+
+    @pl.when(z > 0)
+    def _():
+        hello((p - 4, s))
+
+    @pl.when(z < ZN - 1)
+    def _():
+        hello((p + 4, s))
+
+    ends = jnp.where(z == 0, 1, 0) + jnp.where(z == ZN - 1, 1, 0)
+    pl.semaphore_wait(barrier, 5 - ends)
+
+
+def gather_kernel(nq, nk, *refs):
+    src = refs[:nq]
+    out = refs[nq : 2 * nq]
+    send_sem, recv_sem, psend_sem, precv_sem, own_sem = refs[2 * nq :]
+    p, z, y, x, s = place()
+
+    def span(q, k, side):
+        half = src[q].shape[0] // 2
+        low, high = half * k // nk, half * (k + 1) // nk
+        return pl.ds(side * half + low, high - low)
+
+    def rows(q, k):
+        return span(q, k, s)
+
+    def far_rows(q, k):
+        return span(q, k, 1 - s)
+
+    def dest(way):
+        if way == "u":
+            return p + 4
+        if way == "d":
+            return p - 4
+        return p ^ 1 if way == "x" else p ^ 2
+
+    LANE = {"u": 0, "d": 1, "x": 2, "y": 3}
+
+    def copy(q, k, origin, way, own):
+        block = src[q].at[rows(q, k)] if own else out[q].at[origin, rows(q, k)]
+        return pltpu.make_async_remote_copy(
+            src_ref=block,
+            dst_ref=out[q].at[origin, rows(q, k)],
+            send_sem=send_sem.at[LANE[way], q, k, origin],
+            recv_sem=recv_sem.at[q, k, origin],
+            device_id=(dest(way), s),
+            device_id_type=MESH,
+        )
+
+    def arrive(q, k, origin):
+        pltpu.make_async_remote_copy(
+            src_ref=out[q].at[origin, rows(q, k)],
+            dst_ref=out[q].at[origin, rows(q, k)],
+            send_sem=send_sem.at[0, q, k, origin],
+            recv_sem=recv_sem.at[q, k, origin],
+            device_id=(p, s),
+            device_id_type=MESH,
+        ).wait_recv()
+
+    def hand(q, k, origin):
+        return pltpu.make_async_remote_copy(
+            src_ref=out[q].at[origin, rows(q, k)],
+            dst_ref=out[q].at[origin, rows(q, k)],
+            send_sem=psend_sem.at[q, k, origin],
+            recv_sem=precv_sem.at[q, k, origin],
+            device_id=(p, 1 - s),
+            device_id_type=MESH,
+        )
+
+    greet(p, z, s)
+    pieces = [(q, k) for q in range(nq) for k in range(nk)]
+    first = lambda k: "x" if k % 2 == 0 else "y"
+    second = lambda k: "y" if k % 2 == 0 else "x"
+    log = []
+
+    def go(cond, fn):
+        if cond is None:
+            fn()
+        else:
+            pl.when(cond)(fn)
+
+    def start(cond, c):
+        go(cond, c.start)
+        log.append((cond, c.wait_send))
+
+    def both(a, b):
+        return b if a is None else a & b
+
+    for q, k in pieces:
+        start(z < ZN - 1, copy(q, k, p, "u", True))
+        start(z > 0, copy(q, k, p, "d", True))
+        start(None, copy(q, k, p, first(k), True))
+        start(None, copy(q, k, p, second(k), True))
+    owned = [pltpu.make_async_copy(src[q], out[q].at[p], own_sem.at[q]) for q in range(nq)]
+    for c in owned:
+        c.start()
+
+    offsets = [0]
+    for d in range(1, ZN):
+        offsets += [-d, d]
+    for q in range(nq):
+        for d in offsets:
+            ok = None if d == 0 else ((z + d >= 0) & (z + d < ZN))
+            o = p + 4 * d
+            for k in range(nk):
+                if d != 0:
+                    def relay(k=k, o=o, d=d):
+                        arrive(q, k, o)
+
+                    go(ok, relay)
+                    if d < 0:
+                        start(both(ok, z < ZN - 1), copy(q, k, o, "u", False))
+                    else:
+                        start(both(ok, z > 0), copy(q, k, o, "d", False))
+                    start(ok, copy(q, k, o, first(k), False))
+                    start(ok, copy(q, k, o, second(k), False))
+                    start(ok, hand(q, k, o))
+            for k in range(nk):
+                o1 = (p ^ (1 if first(k) == "x" else 2)) + 4 * d
+                go(ok, lambda: arrive(q, k, o1))
+                start(ok, copy(q, k, o1, second(k), False))
+                start(ok, hand(q, k, o1))
+            for k in range(nk):
+                o2 = (p ^ (2 if first(k) == "x" else 1)) + 4 * d
+                go(ok, lambda: arrive(q, k, o2))
+                start(ok, hand(q, k, o2))
+            for k in range(nk):
+                o3 = (p ^ 3) + 4 * d
+                go(ok, lambda: arrive(q, k, o3))
+                start(ok, hand(q, k, o3))
+    for c in owned:
+        c.wait()
+    for cond, w in log:
+        go(cond, w)
+    for q in range(nq):
+        for k in range(nk):
+            for flip in range(4):
+                for d in offsets:
+                    if d == 0 and flip == 0:
+                        continue
+                    ok = None if d == 0 else ((z + d >= 0) & (z + d < ZN))
+                    o = (p ^ flip) + 4 * d
+
+                    def take(q=q, k=k, o=o):
+                        pltpu.make_async_remote_copy(
+                            src_ref=out[q].at[o, far_rows(q, k)],
+                            dst_ref=out[q].at[o, far_rows(q, k)],
+                            send_sem=psend_sem.at[q, k, o],
+                            recv_sem=precv_sem.at[q, k, o],
+                            device_id=(p, 1 - s),
+                            device_id_type=MESH,
+                        ).wait_recv()
+
+                    go(ok, take)
+
+
+def gather_all(shards, dp, cid, nk=2):
+    nq = len(shards)
+    shapes = [jax.ShapeDtypeStruct((dp,) + shard.shape, shard.dtype) for shard in shards]
+    return pl.pallas_call(
+        functools.partial(gather_kernel, nq, nk),
+        out_shape=shapes,
+        in_specs=[pl.BlockSpec(memory_space=pltpu.VMEM)] * nq,
+        out_specs=[pl.BlockSpec(memory_space=pl.ANY)] * nq,
+        scratch_shapes=[
+            pltpu.SemaphoreType.DMA((4, nq, nk, dp)),
+            pltpu.SemaphoreType.DMA((nq, nk, dp)),
+            pltpu.SemaphoreType.DMA((nq, nk, dp)),
+            pltpu.SemaphoreType.DMA((nq, nk, dp)),
+            pltpu.SemaphoreType.DMA((nq,)),
+        ],
+        compiler_params=pltpu.CompilerParams(
+            collective_id=cid, has_side_effects=True, vmem_limit_bytes=60 * 2**20
+        ),
+        name="gather_all",
+    )(*shards)
+
+
+def scatter_kernel(cuts, g_ref, note_ref, out_ref, tot_ref, acc, pr, r1, r2, ru, rd,
+                   sbuf, rbuf, zbuf, loc_sem, pair_s, pair_r, d1_s, d1_r, d2_s, d2_r,
+                   up_s, up_r, dn_s, dn_r, fin_s, fin_r, sc_s, sc_r, zu_s, zu_r, zd_s, zd_r):
+    p, z, y, x, s = place()
+    H = cuts[-1]
+    over = 2 * H - out_ref.shape[0]
+    base = s * (H - over)
+    far = (1 - s) * (H - over)
+    nk = len(cuts) - 1
+
+    def rows(k, first=0):
+        return pl.ds(first + cuts[k], cuts[k + 1] - cuts[k])
+
+    def remote(src, dst, a, b, dev):
+        return pltpu.make_async_remote_copy(src_ref=src, dst_ref=dst, send_sem=a, recv_sem=b,
+                                            device_id=dev, device_id_type=MESH)
+
+    def load(k):
+        return pltpu.make_async_copy(g_ref.at[:, :, :, rows(k, base)],
+                                     acc.at[:, :, :, rows(k)], loc_sem.at[k])
+
+    def pair(k):
+        return remote(g_ref.at[:, :, :, rows(k, far)], pr.at[:, :, :, rows(k)],
+                      pair_s.at[k], pair_r.at[k], (p, 1 - s))
+
+    def one(k):
+        if k % 2 == 0:
+            src, dst, dev = acc.at[:, :, 1 - x, rows(k)], r1.at[:, :, rows(k)], (p ^ 1, s)
+        else:
+            src, dst, dev = acc.at[:, 1 - y, :, rows(k)], r1.at[:, :, rows(k)], (p ^ 2, s)
+        return remote(src, dst, d1_s.at[k], d1_r.at[k], dev)
+
+    def two(k):
+        if k % 2 == 0:
+            src, dev = acc.at[:, 1 - y, x, rows(k)], (p ^ 2, s)
+        else:
+            src, dev = acc.at[:, y, 1 - x, rows(k)], (p ^ 1, s)
+        return remote(src, r2.at[:, rows(k)], d2_s.at[k], d2_r.at[k], dev)
+
+    def up(k, t):
+        return remote(acc.at[t, y, x, rows(k)], ru.at[t, rows(k)], up_s.at[k, t], up_r.at[k, t],
+                      (p + 4, s))
+
+    def down(k, t):
+        return remote(acc.at[t, y, x, rows(k)], rd.at[t, rows(k)], dn_s.at[k, t], dn_r.at[k, t],
+                      (p - 4, s))
+
+    def add_up(k, t):
+        acc[t, y, x, rows(k)] += ru[t, rows(k)]
+
+    def add_down(k, t):
+        acc[t, y, x, rows(k)] += rd[t, rows(k)]
+
+    greet(p, z, s)
+    for k in range(nk):
+        pair(k).start()
+        load(k).start()
+
+    def stage_pair(k):
+        load(k).wait()
+        pair(k).wait_recv()
+
+        def body(i, c):
+            a, b, d = i // 4, (i // 2) % 2, i % 2
+            acc[a, b, d, rows(k)] += pr[a, b, d, rows(k)]
+            return c
+
+        lax.fori_loop(0, 16, body, 0)
+        one(k).start()
+
+    def stage_one(k):
+        one(k).wait_recv()
+
+        def body(i, c):
+            a, b = i // 2, i % 2
+            if k % 2 == 0:
+                acc[a, b, x, rows(k)] += r1[a, b, rows(k)]
+            else:
+                acc[a, y, b, rows(k)] += r1[a, b, rows(k)]
+            return c
+
+        lax.fori_loop(0, 8, body, 0)
+        two(k).start()
+
+    def stage_two(k):
+        two(k).wait_recv()
+
+        def body(a, c):
+            acc[a, y, x, rows(k)] += r2[a, rows(k)]
+            return c
+
+        lax.fori_loop(0, 4, body, 0)
+
+        @pl.when(z == 0)
+        def _():
+            for t in range(ZN - 1, 0, -1):
+                up(k, t).start()
+
+        @pl.when(z == ZN - 1)
+        def _():
+            for t in range(ZN - 1):
+                down(k, t).start()
+
+    def stage_z(k, i):
+        t = ZN - 1 - i
+
+        @pl.when((z > 0) & (z < t))
+        def _():
+            up(k, t).wait_recv()
+            add_up(k, t)
+            up(k, t).start()
+
+        @pl.when((z < ZN - 1) & (z > i))
+        def _():
+            down(k, i).wait_recv()
+            add_down(k, i)
+            down(k, i).start()
+
+    def stage_last(k):
+        @pl.when(z > 0)
+        def _():
+            up(k, z).wait_recv()
+            add_up(k, z)
+
+        @pl.when(z < ZN - 1)
+        def _():
+            down(k, z).wait_recv()
+            add_down(k, z)
+
+    stages = [stage_pair, stage_one, stage_two] + [
+        functools.partial(lambda i, k: stage_z(k, i), i) for i in range(ZN - 1)
+    ] + [stage_last]
+    for t in range(nk + len(stages) - 1):
+        for j in range(len(stages)):
+            if 0 <= t - j < nk:
+                stages[j](t - j)
+
+    low = lambda: remote(acc.at[z, y, x, pl.ds(0, H)], out_ref.at[pl.ds(0, H)],
+                         fin_s, fin_r, (p, 1 - s))
+    high = lambda: remote(acc.at[z, y, x, pl.ds(over, H - over)],
+                          out_ref.at[pl.ds(H, H - over)], fin_s, fin_r, (p, 1 - s))
+
+    @pl.when(s == 0)
+    def _():
+        low().start()
+        out_ref[pl.ds(0, H)] = acc[z, y, x, pl.ds(0, H)]
+
+    @pl.when(s == 1)
+    def _():
+        high().start()
+        out_ref[pl.ds(H, H - over)] = acc[z, y, x, pl.ds(over, H - over)]
+
+    mine = acc[z, y, x, pl.ds(over, H - over)]
+    sq = jnp.sum(mine * mine)
+    for i in range(over):
+        head = acc[z, y, x, i]
+        sq = sq + jnp.where(s == 0, jnp.sum(head * head), 0.0)
+    row = lax.broadcasted_iota(jnp.int32, (8, 128), 0)
+    cur = jnp.where(row == 1, sq, note_ref[...])
+    for j, dev in enumerate([(p, 1 - s), (p ^ 1, s), (p ^ 2, s)]):
+        sbuf[j] = cur
+        c = remote(sbuf.at[j], rbuf.at[j], sc_s.at[j], sc_r.at[j], dev)
+        c.start()
+        c.wait()
+        cur = cur + rbuf[j]
+    zbuf[z] = cur
+
+    def zup(o):
+        return remote(zbuf.at[o], zbuf.at[o], zu_s.at[o], zu_r.at[o], (p + 4, s))
+
+    def zdn(o):
+        return remote(zbuf.at[o], zbuf.at[o], zd_s.at[o], zd_r.at[o], (p - 4, s))
+
+    @pl.when(z < ZN - 1)
+    def _():
+        zup(z).start()
+
+    @pl.when(z > 0)
+    def _():
+        zdn(z).start()
+
+    for d in range(1, ZN):
+        @pl.when(z - d >= 0)
+        def _():
+            zup(z - d).wait_recv()
+
+        @pl.when((z - d >= 0) & (z < ZN - 1))
+        def _():
+            zup(z - d).start()
+
+        @pl.when(z + d < ZN)
+        def _():
+            zdn(z + d).wait_recv()
+
+        @pl.when((z + d < ZN) & (z > 0))
+        def _():
+            zdn(z + d).start()
+
+    total = zbuf[0]
+    for i in range(1, ZN):
+        total = total + zbuf[i]
+    tot_ref[...] = total
+
+    @pl.when(s == 0)
+    def _():
+        low().wait_send()
+        high().wait_recv()
+
+    @pl.when(s == 1)
+    def _():
+        high().wait_send()
+        low().wait_recv()
+
+    for k in range(nk):
+        pair(k).wait_send()
+        one(k).wait_send()
+        two(k).wait_send()
+        for t in range(ZN):
+            @pl.when(z < t)
+            def _():
+                up(k, t).wait_send()
+
+            @pl.when(z > t)
+            def _():
+                down(k, t).wait_send()
+    for o in range(ZN):
+        @pl.when((o <= z) & (z < ZN - 1))
+        def _():
+            zup(o).wait_send()
+
+        @pl.when((o >= z) & (z > 0))
+        def _():
+            zdn(o).wait_send()
+
+
+def scatter_all(grads, note, cid, nk=6):
+    dp, tiles = grads.shape[0], grads.shape[1]
+    H = (tiles + 1) // 2
+    cuts = [H * i // nk for i in range(nk + 1)]
+    dma = pltpu.SemaphoreType.DMA
+    box = (8, D)
+    return pl.pallas_call(
+        functools.partial(scatter_kernel, cuts),
+        out_shape=[
+            jax.ShapeDtypeStruct((tiles,) + box, jnp.float32),
+            jax.ShapeDtypeStruct((8, 128), jnp.float32),
+        ],
+        in_specs=[pl.BlockSpec(memory_space=pl.ANY), pl.BlockSpec(memory_space=pltpu.VMEM)],
+        out_specs=[pl.BlockSpec(memory_space=pltpu.VMEM)] * 2,
+        scratch_shapes=[
+            pltpu.VMEM((ZN, 2, 2, H) + box, jnp.float32),
+            pltpu.VMEM((ZN, 2, 2, H) + box, jnp.float32),
+            pltpu.VMEM((ZN, 2, H) + box, jnp.float32),
+            pltpu.VMEM((ZN, H) + box, jnp.float32),
+            pltpu.VMEM((ZN, H) + box, jnp.float32),
+            pltpu.VMEM((ZN, H) + box, jnp.float32),
+            pltpu.VMEM((3, 8, 128), jnp.float32),
+            pltpu.VMEM((3, 8, 128), jnp.float32),
+            pltpu.VMEM((ZN, 8, 128), jnp.float32),
+            dma((nk,)), dma((nk,)), dma((nk,)), dma((nk,)), dma((nk,)), dma((nk,)), dma((nk,)),
+            dma((nk, ZN)), dma((nk, ZN)), dma((nk, ZN)), dma((nk, ZN)),
+            dma, dma, dma((3,)), dma((3,)), dma((ZN,)), dma((ZN,)), dma((ZN,)), dma((ZN,)),
+        ],
+        compiler_params=pltpu.CompilerParams(
+            collective_id=cid, has_side_effects=True, vmem_limit_bytes=67043328
+        ),
+        name="scatter_all",
+    )(grads.reshape((ZN, 2, 2, tiles) + box), note)
 
 
 def layout():
@@ -305,13 +779,31 @@
     second_moment,
     step_count,
 ):
-    gathered, teacher_all = (
-        lax.all_gather(weights.astype(jnp.bfloat16), "dp", axis=0, tiled=True),
-        lax.all_gather(teacher, "dp", axis=0, tiled=True),
-    )
+    dp = lax.axis_size("dp")
+    own_kernels = dp == 4 * ZN
+    chip_count = jnp.sum((block_masks == 1).astype(jnp.float32))
+    blocks_in = lambda rows: rows.reshape(-1, CR, D)
+    if own_kernels:
+        gathered, teacher_all, counts = gather_all(
+            [
+                blocks_in(weights.astype(jnp.bfloat16)),
+                blocks_in(teacher),
+                jnp.broadcast_to(chip_count, (4, 8, 128)),
+            ],
+            dp,
+            1,
+        )
+        masked_count = jnp.sum(counts[:, 0, 0, 0])
+        gathered, teacher_all = (gathered.reshape(-1, CR, D), teacher_all.reshape(-1, CR, D))
+    else:
+        gathered, teacher_all = (
+            blocks_in(lax.all_gather(weights.astype(jnp.bfloat16), "dp", axis=0, tiled=True)),
+            blocks_in(lax.all_gather(teacher, "dp", axis=0, tiled=True)),
+        )
+        masked_count = lax.psum(chip_count, "dp")
     inverse_order = jnp.argsort(span_order)
-    params = unpack(reorder(gathered, inverse_order))
-    teacher_params = unpack(reorder(teacher_all, inverse_order))
+    params = unpack(gathered[inverse_order].reshape(-1, D))
+    teacher_params = unpack(teacher_all[inverse_order].reshape(-1, D))
     seq_side = lax.axis_index("seq")
     is_patch, is_cls, grid_cell = slot_info(split_rows, seq_side)
     far_patch, far_cls, far_cell = slot_info(split_rows, 1 - seq_side)
@@ -320,7 +812,6 @@
     images = patches.shape[0]
     hidden_mask = (jnp.take_along_axis(block_masks, grid_cell, 1) == 1) & is_patch
     key_live = is_patch | is_cls
-    masked_count = lax.psum(jnp.sum(hidden_mask.astype(jnp.float32)), ("dp", "seq"))
     position = sincos(grid_cell)
     pixels = patches.reshape(-1, PP)
     embedded_teacher = matmul_f32(pixels, teacher_params["w_pe"]) + vector(teacher_params, "b_pe")
@@ -361,9 +852,7 @@
     )
     selected = hidden_mask.reshape(-1)[:, None]
     loss_scale = 1.0 / (math.sqrt(D) * masked_count)
-    total_loss = lax.psum(
-        jnp.sum(jnp.where(selected, elementwise, 0.0)) * loss_scale, ("dp", "seq")
-    )
+    part_loss = jnp.sum(jnp.where(selected, elementwise, 0.0)) * loss_scale
     grad_pred = (
         jnp.where(selected, jnp.clip(difference / BETA, -1.0, 1.0), 0.0) * loss_scale
     ).astype(jnp.bfloat16)
@@ -383,9 +872,17 @@
     gradients["mask_tok"] = jnp.sum(jnp.where(hidden_mask[..., None], grad_slots, 0.0), (0, 1))
     gradients["cls"] = jnp.sum(jnp.where(is_cls[..., None], grad_slots, 0.0), (0, 1))
     stored_grad = reorder(pack_flat(gradients, span_order.shape[0] * CR), span_order)
-    owned_grad = lax.psum_scatter(stored_grad, "dp", scatter_dimension=0, tiled=True)
-    owned_grad = lax.psum(owned_grad, "seq")
-    squares = lax.psum(jnp.sum(owned_grad * owned_grad), "dp")
+    if own_kernels:
+        owned_grad, totals = scatter_all(
+            stored_grad.reshape(dp, -1, 8, D), jnp.broadcast_to(part_loss, (8, 128)), 2
+        )
+        owned_grad = owned_grad.reshape(-1, D)
+        total_loss, squares = (totals[0, 0], totals[1, 0])
+    else:
+        owned_grad = lax.psum_scatter(stored_grad, "dp", scatter_dimension=0, tiled=True)
+        owned_grad = lax.psum(owned_grad, "seq")
+        total_loss = lax.psum(part_loss, ("dp", "seq"))
+        squares = lax.psum(jnp.sum(owned_grad * owned_grad), "dp")
     grad_norm = jnp.sqrt(squares)
     clipped = owned_grad * (CLIP / jnp.maximum(grad_norm, CLIP))
     updated_first = BETA_ONE * first_moment + (1.0 - BETA_ONE) * clipped

time: 1550 us -> 962 us (0.62)
  waiting for transfers between devices: 754 us -> 0.01 us
  Pallas kernels: 0 us -> 403 us
  blocking collectives: 126 us -> 0 us
  local copies, waits for them, and re-layouts: 512 us -> 423 us
    reduce_scatter x1 -> x0, waiting for transfers between devices: 495 us -> none  [on_device(): lax.psum_scatter(stored_grad, 'dp', scatter_dimension=0, tiled=True)]
    pallas_call x0 -> x2, Pallas kernels: none -> 403 us  [the longest x1 216 us: scatter_all(): pl.pallas_call(functools.partial(scatter_kernel, cuts), out_shape=[jax.Sh...]
    all_gather x2 -> x0, waiting for transfers between devices: 237 us -> none  [the longest x1 135 us: on_device(): lax.all_gather(teacher, 'dp', axis=0, tiled=True)]
    reshape x6 -> x1, local copies, waits for them, and re-layouts: 186 us -> 37.9 us  [reorder(): return stored.reshape(order.shape[0], -1, D)[order].reshape(-1, D)]
    psum x3 -> x0, blocking collectives: 126 us -> none  [the longest x1 44.4 us: on_device(): lax.psum(jnp.sum(hidden_mask.astype(jnp.float32)), ('dp', 'seq'))]
    reshape x0 -> x4, local copies, waits for them, and re-layouts: none -> 55.7 us  [the longest x1 26.7 us: on_device(): teacher_params = unpack(teacher_all[inverse_order].reshape(-1, D))]
    gather x3 -> x1, local copies, waits for them, and re-layouts: 85.2 us -> 32.5 us  [reorder(): return stored.reshape(order.shape[0], -1, D)[order].reshape(-1, D)]
    gather x0 -> x2, local copies, waits for them, and re-layouts: none -> 52.6 us  [the longest x1 26.4 us: on_device(): teacher_params = unpack(teacher_all[inverse_order].reshape(-1, D))]
  transfers between devices with their start and end apart: 6 -> 2, of which waited for: 4 -> 0; matrix products, arithmetic and copies ran while one was open for 12% -> 10% of each run, Pallas kernels for 0% -> 0%
where the time goes in v1:
time: 962 us; the launch traced here: 950 us
  local copies, waits for them, and re-layouts  423 us (44%)
  Pallas kernels  403 us (42%)
  matrix products  78.7 us (8%)
  other arithmetic  37.5 us (4%)
    pallas_call x1, Pallas kernels, scatter_all(): pl.pallas_call(functools.partial(scatter_kernel, cuts), out_shape=[jax.Sh...  216 us
    pallas_call x1, Pallas kernels, gather_all(): pl.pallas_call(functools.partial(gather_kernel, nq, nk), out_shape=shapes...  187 us
    concatenate x1, local copies, waits for them, and re-layouts, pack_flat(): jnp.concatenate([stacked, jnp.zeros((total_rows - stacked.shape[0], D), s...  78.5 us
    slice x15, local copies, waits for them, and re-layouts, unpack(): tables[entry_name] = flat[offset:offset + entry_rows].reshape(entry_shape)  53.3 us
    another operation x1, local copies, waits for them, and re-layouts, scatter_all(): grads.reshape((ZN, 2, 2, tiles) + box)  38.5 us
    reshape x1, local copies, waits for them, and re-layouts, reorder(): return stored.reshape(order.shape[0], -1, D)[order].reshape(-1, D)  37.9 us
    gather x1, local copies, waits for them, and re-layouts, reorder(): return stored.reshape(order.shape[0], -1, D)[order].reshape(-1, D)  32.5 us
    reshape x15, local copies, waits for them, and re-layouts, pack_flat(): tables[entry_name].reshape(-1, D)  30.6 us
  transfers between devices with their start and end apart: 2, of which 0 were waited for; matrix products, arithmetic and copies ran while one was open for 10% of the time, Pallas kernels for 0%

profile of v1, /device:TPU:0, one launch (start us, length us, event | category | flops | bytes accessed | tf_op | source)
XLA Modules:
  0.0 949.9 jit_solution(8947610043135397134)
XLA Ops:
  2.7 1.8 convert_element_type.232
  7.6 5.8 sort.17
  14.6 187.2 %gather_all.1 = (bf16[16,170,4,768]{3,2,1,0:T(4,128)(2,1)}, bf16[16,170,4,768]{3,2,1,0:T(4,128)(2,1)}, f32[16,4,8,128]{3,2,1,0:T(8,128)}) custom-call(bf16[170,4,768]{2,1,0:T(4,128)(2,1)} %reshape.818.refs_0_, bf16[170,4,768]{2,1,0:T(4,128)(2,1)} %reshape.819.refs_1_, f32[4,8,128]{2,1,0:T(8,128)} %broadcast_in_dim.212.refs_2_), custom_call_target="tpu_custom_call" | custom-call | tf_op jit(solution)/shard_map/gather_all/pallas_call | solution.py:217
  201.8 26.4 %gather_fusion.1 = bf16[2720,4,768]{2,1,0:T(4,128)(2,1)} fusion(bf16[2720,4,768]{2,1,0:T(4,128)(2,1)} %bitcast.307, s32[3072]{0:T(1024)S(1)} %pad_clamp_fusion.1), kind=kCustom, calls=%fused_computation.1 | custom fusion | bytes 33434240 | tf_op jit(solution)/shard_map/gather | solution.py:806
  228.2 26.7 %reshape.826 = bf16[10880,768]{1,0:T(8,128)(2,1)} reshape(bf16[2720,4,768]{2,1,0:T(4,128)(2,1)} %gather_fusion.1) | data formatting | bytes 33423360 | tf_op jit(solution)/shard_map/reshape | solution.py:806
  254.9 3.5 fusion.167
  258.3 26.1 %gather_fusion = bf16[2720,4,768]{2,1,0:T(4,128)(2,1)} fusion(bf16[2720,4,768]{2,1,0:T(4,128)(2,1)} %bitcast.306, s32[3072]{0:T(1024)S(1)} %pad_clamp_fusion.1), kind=kCustom, calls=%fused_computation | custom fusion | bytes 33434240 | tf_op jit(solution)/shard_map/gather | solution.py:805
  284.5 26.7 %reshape.821 = bf16[10880,768]{1,0:T(8,128)(2,1)} reshape(bf16[2720,4,768]{2,1,0:T(4,128)(2,1)} %gather_fusion) | data formatting | bytes 33423360 | tf_op jit(solution)/shard_map/reshape | solution.py:805
  311.1 4.6 fusion.165
  315.7 2.5 gather_fusion.3
  318.2 1.6 fusion.112
  321.5 1.9 multiply_sine_fusion.1
  324.3 2.2 fusion.171
  327.7 4.0 reshape.827
  331.7 3.4 convolution_convert_fusion
  340.1 1.8 fusion.116
  343.0 2.5 fusion.173
  346.7 4.0 reshape.823
  350.7 3.4 convolution_convert_fusion.1
  355.3 2.0 fusion.168
  359.0 10.6 %fusion.166 = (bf16[768,4,768]{2,1,0:T(4,128)(2,1)}, bf16[768,4,768]{2,1,0:T(4,128)(2,1)}) fusion(bf16[2720,4,768]{2,1,0:T(4,128)(2,1)} %gather_fusion.1), kind=kLoop, calls=%fused_computation.335 | loop fusion | bytes 18874368 | tf_op jit(solution)/shard_map/slice | solution.py:534
  370.3 10.7 %fusion.164 = (bf16[768,4,768]{2,1,0:T(4,128)(2,1)}, bf16[768,4,768]{2,1,0:T(4,128)(2,1)}) fusion(bf16[2720,4,768]{2,1,0:T(4,128)(2,1)} %gather_fusion), kind=kLoop, calls=%fused_computation.333 | loop fusion | bytes 18874368 | tf_op jit(solution)/shard_map/slice | solution.py:534
  382.2 5.5 copy.83
  387.7 8.6 slice.220
  398.1 5.6 copy.81
  405.0 8.6 slice.202
  421.1 1.7 fusion.177
  429.5 7.3 fusion.176
  437.6 1.7 fusion.178
  443.2 4.0 convolution_add_fusion.1
  447.3 2.2 fusion.180
  451.4 2.1 fusion.159
  455.6 3.8 convert_reduce_fusion
  459.4 5.1 fusion.158
  464.5 2.2 multiply_reduce_fusion.3
  467.6 1.9 fusion.65
  474.1 1.8 multiply_reduce_fusion
  480.8 11.8 %reshape.849 = f32[3072,768]{1,0:T(8,128)} reshape(f32[768,3072]{1,0:T(8,128)} %fusion.158) | data formatting | bytes 18874368 | tf_op jit(solution)/shard_map/reshape | solution.py:540
  505.2 7.7 fusion.147
  517.2 4.2 fusion.43
  522.8 8.5 reshape.848
  532.3 2.1 convolution_bitcast_fusion
  534.5 78.5 %concatenate.9 = f32[10880,768]{1,0:T(8,128)} concatenate(f32[1,768]{1,0:T(1,128)S(1)} %reshape.834, f32[1,768]{1,0:T(1,128)S(1)} %reshape.835, f32[1,768]{1,0:T(1,128)S(1)} %reshape.836, f32[1,768]{1,0:T(1,128)S(1)} %reshape.837, f32[1,768]{1,0:T(1,128)S(1)} %reshape.838, f32[1,768]{1,0:T(1,128)S(1)} %copy-done.63, f32[1,768]{1,0:T(1,128)S(1)} %copy-done.64, ...), dimensions={0} | concatenate | bytes 66846720 | tf_op jit(solution)/shard_map/concatenate | solution.py:542
  613.0 37.9 %reshape.850 = f32[2720,4,768]{2,1,0:T(4,128)} reshape(f32[10880,768]{1,0:T(8,128)} %concatenate.9) | data formatting | bytes 66846720 | tf_op jit(solution)/shard_map/reshape | solution.py:548
  650.8 32.5 %gather_fusion.2 = f32[2720,4,768]{2,1,0:T(4,128)} fusion(f32[2720,4,768]{2,1,0:T(4,128)} %reshape.850, s32[3072]{0:T(1024)S(1)} %copy-done.51), kind=kCustom, calls=%fused_computation.2 | custom fusion | bytes 66857600 | tf_op jit(solution)/shard_map/gather | solution.py:548
  683.4 38.5 %reshape_reshape_reshape.3.g_ref = f32[4,2,2,85,8,768]{5,4,3,2,1,0:T(8,128)} reshape(f32[2720,4,768]{2,1,0:T(4,128)} %gather_fusion.2) | data formatting | bytes 66846720 | tf_op jit(solution)/shard_map/reshape;reshape;reshape | solution.py:503
  722.5 216.3 %scatter_all.1 = (f32[85,8,768]{2,1,0:T(8,128)}, f32[8,128]{1,0:T(8,128)}) custom-call(f32[4,2,2,85,8,768]{5,4,3,2,1,0:T(8,128)} %reshape_reshape_reshape.3.g_ref, f32[8,128]{1,0:T(8,128)} %broadcast_in_dim.231.note_ref), custom_call_target="tpu_custom_call" | custom-call | tf_op jit(solution)/shard_map/scatter_all/pallas_call | solution.py:477
  940.8 7.5 fusion.160
  (331 shorter events, 76.4 us)
Async XLA Ops:
  0.7 322.8 %copy-start.85 = (pred[128]{0:T(512)(128)(4,1)}, pred[128]{0:T(512)(128)(4,1)S(1)}, u32[]{:S(2)}) copy-start(pred[128]{0:T(512)(128)(4,1)S(1)} %compare_and_fusion.3) | copy-start | bytes 388
  0.7 322.8 %copy-start.76 = (pred[128]{0:T(512)(128)(4,1)}, pred[128]{0:T(512)(128)(4,1)S(1)}, u32[]{:S(2)}) copy-start(pred[128]{0:T(512)(128)(4,1)S(1)} %iota_compare_fusion.1) | copy-start | bytes 388
  1.4 322.1 %copy-start.87 = (pred[2]{0:T(512)(128)(4,1)}, pred[2]{0:T(512)(128)(4,1)S(1)}, u32[]{:S(2)}) copy-start(pred[2]{0:T(512)(128)(4,1)S(1)} %broadcast_compare_fusion) | copy-start | bytes 10
  2.5 321.0 %copy-start.74 = (s32[2]{0:T(128)}, s32[2]{0:T(128)S(1)}, u32[]{:S(2)}) copy-start(s32[2]{0:T(128)S(1)} %get-tuple-element.105) | copy-start | bytes 28
  2.5 321.0 %copy-start.78 = (s32[2]{0:T(128)}, s32[2]{0:T(128)S(1)}, u32[]{:S(2)}) copy-start(s32[2]{0:T(128)S(1)} %get-tuple-element.104) | copy-start | bytes 28
  318.2 6.1 copy-start.72
  323.4 3.1 copy-start.41
  323.4 3.1 copy-start.42
  323.4 3.1 copy-start.43
  324.3 3.3 slice-start.1
  336.0 5.9 copy-start.18
  341.9 8.8 copy-start.46
  341.9 8.8 copy-start.49
  343.0 3.6 slice-start
  345.6 5.1 copy-start.56
  346.7 4.0 copy-start.58
  357.3 82.7 %copy-start.14 = (bf16[2,128,1,12,64]{1,0,4,3,2:T(2,128)(2,1)}, bf16[2,128,1,12,64]{1,0,4,3,2:T(2,128)(2,1)S(1)}, u32[]{:S(2)}) copy-start(bf16[2,128,1,12,64]{1,0,4,3,2:T(2,128)(2,1)S(1)} %get-tuple-element.83) | copy-start | bytes 1179652
  358.8 63.9 %collective-permute-start = (bf16[4,2,128,12,64]{2,4,3,1,0:T(8,128)(2,1)}, bf16[4,2,128,12,64]{2,4,3,1,0:T(8,128)(2,1)}, u32[]{:S(2)}, u32[]{:S(2)}) collective-permute-start(bf16[4,2,128,12,64]{2,4,3,1,0:T(8,128)(2,1)} %pad_maximum_fusion), channel_id=1, source_target_pairs={{0,1},{1,0},{2,3},{3,2},{4,5},{5,4},{6,7},{7,6},{8,9},{9,8},{10,11... | collective-permute-start | bytes 4718600 | tf_op jit(solution)/shard_map/ppermute | solution.py:32
  370.3 10.8 %copy-start.19 = (bf16[192,4,768]{2,1,0:T(4,128)(2,1)S(1)}, bf16[192,4,768]{2,1,0:T(4,128)(2,1)}, u32[]{:S(2)}) copy-start(bf16[192,4,768]{2,1,0:T(4,128)(2,1)} %get-tuple-element.80) | copy-start | bytes 3538948
  387.7 9.2 copy-start.17
  405.0 8.7 copy-start.16
  413.6 4.6 copy-start.53
  413.6 5.2 copy-start.73
  413.6 5.2 copy-start.75
  413.6 5.2 copy-start.77
  413.6 5.2 copy-start.79
  413.6 5.2 copy-start.86
  413.6 5.2 copy-start.88
  413.7 5.2 copy-start.89
  413.7 5.8 copy-start.32
  419.5 3.3 copy-start.96
  419.5 3.3 copy-start.39
  442.9 4.3 slice-start.4
  443.2 4.0 slice-start.5
  443.2 4.0 copy-start.84
  447.2 8.4 copy-start.15
  454.7 9.8 %slice-start.2 = ((s8[4718592]{0:T(1024)(128)(4,1)}), s8[4194304]{0:T(1024)(128)(4,1)S(1)}, s32[]{:S(2)}) async-start(s8[4718592]{0:T(1024)(128)(4,1)} %bitcast.309), calls=%async_computation.2 | async-start | bytes 8388608
  455.6 11.1 %copy-start.8 = (f32[256,768]{1,0:T(8,128)}, f32[256,768]{1,0:T(8,128)S(1)}, u32[]{:S(2)}) copy-start(f32[256,768]{1,0:T(8,128)S(1)} %get-tuple-element.66) | copy-start | bytes 2359300
  455.6 8.9 slice-start.3
  479.2 33.7 %collective-permute-start.1 = (bf16[2,2,128,12,64]{2,4,3,1,0:T(8,128)(2,1)}, bf16[2,2,128,12,64]{2,4,3,1,0:T(8,128)(2,1)}, u32[]{:S(2)}, u32[]{:S(2)}) collective-permute-start(bf16[2,2,128,12,64]{2,4,3,1,0:T(8,128)(2,1)} %pad_maximum_fusion.2), channel_id=1, source_target_pairs={{0,1},{1,0},{2,3},{3,2},{4,5},{5,4},{6,7},{7,6},{8,9},{9,8},{10,11... | collective-permute-start | bytes 2359304 | tf_op jit(solution)/shard_map/ppermute | solution.py:32
  480.8 22.8 %copy-start.11 = (bf16[2,12,128,128]{2,3,1,0:T(8,128)(2,1)S(1)}, bf16[2,12,128,128]{2,3,1,0:T(8,128)(2,1)}, u32[]{:S(2)}) copy-start(bf16[2,12,128,128]{2,3,1,0:T(8,128)(2,1)} %copy-done.10) | copy-start | bytes 2359300
  492.6 12.6 %copy-start.9 = (f32[256,768]{1,0:T(8,128)S(1)}, f32[256,768]{1,0:T(8,128)}, u32[]{:S(2)}) copy-start(f32[256,768]{1,0:T(8,128)} %copy-done.8) | copy-start | bytes 2359300
  517.2 4.2 copy-start.21
  522.7 8.5 copy-start.5
  522.8 8.5 copy-start.90
  522.8 8.5 copy-start.91
  522.8 8.5 copy-start.93
  613.0 37.9 %copy-start.51 = (s32[3072]{0:T(1024)S(1)}, s32[3072]{0:T(1024)}, u32[]{:S(2)}) copy-start(s32[3072]{0:T(1024)} %pad_clamp_fusion) | copy-start | bytes 36868
  (58 other events, 111.4 us)

commit v2 on v1

--- a/solution.py
+++ b/solution.py
@@ -503,49 +503,152 @@
     )(grads.reshape((ZN, 2, 2, tiles) + box), note)
 
 
-def layout():
-    return [
-        ("cls", 1, (D,)),
-        ("mask_tok", 1, (D,)),
-        ("b_pe", 1, (D,)),
-        ("ln1_g", 1, (D,)),
-        ("ln1_b", 1, (D,)),
-        ("b_out", 1, (D,)),
-        ("ln2_g", 1, (D,)),
-        ("ln2_b", 1, (D,)),
-        ("b_two", 1, (D,)),
-        ("lnf_g", 1, (D,)),
-        ("lnf_b", 1, (D,)),
-        ("b_head", 1, (D,)),
-        ("b_one", FF // D, (FF,)),
-        ("w_pe", PP, (PP, D)),
-        ("w_qkv", 3 * D, (D, 3 * D)),
-        ("w_out", D, (D, D)),
-        ("w_one", FF, (D, FF)),
-        ("w_two", FF, (FF, D)),
-        ("w_head", D, (D, D)),
-    ]
-
-
-def unpack(flat):
-    tables = {}
-    offset = 0
-    for entry_name, entry_rows, entry_shape in layout():
-        tables[entry_name] = flat[offset : offset + entry_rows].reshape(entry_shape)
-        offset = offset + entry_rows
+VECTORS = [
+    "cls",
+    "mask_tok",
+    "b_pe",
+    "ln1_g",
+    "ln1_b",
+    "b_out",
+    "ln2_g",
+    "ln2_b",
+    "b_two",
+    "lnf_g",
+    "lnf_b",
+    "b_head",
+]
+NARROW = [("small", 16, 1), ("w_pe", 768, 1), ("w_qkv", 2304, 3), ("w_out", 768, 1),
+          ("w_one", 3072, 4), ("w_two", 3072, 1), ("w_head", 768, 1)]
+LHS_T = (((0,), (0,)), ((), ()))
+
+
+def sort_kernel(inv_ref, g_ref, small, pe, qkv, out, one, two, head, rows, wide):
+    start = 0
+    for (name, count, ways), dst in zip(NARROW, (small, pe, qkv, out, one, two, head)):
+        to = dst if ways == 1 else rows
+
+        def group(i, c, start=start, to=to):
+            for q in range(4):
+                to[i, 4 * q : 4 * q + 4, :] = g_ref[inv_ref[start // 4 + 4 * i + q]]
+            return c
+
+        lax.fori_loop(0, count // 16, group, 0)
+        if ways > 1:
+            def widen(i, c):
+                r = pl.multiple_of(i * 64, 64)
+                full = rows[pl.ds(i * 4, 4)].reshape(64, D).astype(jnp.float32)
+                for n in range(D // 128):
+                    wide[n, pl.ds(r, 64), :] = full[:, 128 * n : 128 * n + 128]
+                return c
+
+            lax.fori_loop(0, count // 64, widen, 0)
+            high = count // ways
+            for w in range(ways):
+                for r in range(0, high, 128):
+                    for n in range(D // 128):
+                        piece = wide[n, pl.ds(r * ways + w, 128, stride=ways), :]
+                        low = w * D + 128 * n
+                        dst[pl.ds(r, 128), low : low + 128] = piece.astype(jnp.bfloat16)
+        start += count
+
+
+def sorted_weights(gathered, inverse):
+    bf = jnp.bfloat16
+    shapes = [(1, 16, D), (48, 16, D), (D, 3 * D), (48, 16, D), (D, FF), (192, 16, D), (48, 16, D)]
+    outs = pl.pallas_call(
+        sort_kernel,
+        out_shape=[jax.ShapeDtypeStruct(s, bf) for s in shapes],
+        in_specs=[pl.BlockSpec(memory_space=pltpu.SMEM), pl.BlockSpec(memory_space=pltpu.VMEM)],
+        out_specs=[pl.BlockSpec(memory_space=pltpu.VMEM)] * 7,
+        scratch_shapes=[pltpu.VMEM((192, 16, D), bf), pltpu.VMEM((D // 128, 3072, 128), jnp.float32)],
+        compiler_params=pltpu.CompilerParams(vmem_limit_bytes=67043328),
+        name="sort_weights",
+    )(inverse, gathered)
+    small = outs[0].reshape(16, D)
+    tables = {name: small[i] for i, name in enumerate(VECTORS)}
+    tables["b_one"] = small[12:].reshape(FF)
+    tables["w_pe"] = outs[1].reshape(D, D)
+    tables["w_qkv"] = outs[2]
+    tables["w_out"] = outs[3].reshape(D, D)
+    tables["w_one"] = outs[4]
+    tables["w_two"] = outs[5].reshape(FF, D)
+    tables["w_head"] = outs[6].reshape(D, D)
     return tables
 
 
-def pack_flat(tables, total_rows):
-    pieces = [tables[entry_name].reshape(-1, D) for entry_name, entry_rows, entry_shape in layout()]
-    stacked = jnp.concatenate(pieces, 0)
-    return jnp.concatenate(
-        [stacked, jnp.zeros((total_rows - stacked.shape[0], D), stacked.dtype)], 0
-    )
-
-
-def reorder(stored, order):
-    return stored.reshape(order.shape[0], -1, D)[order].reshape(-1, D)
+def grad_kernel(order_ref, small, px, ge, a, gq, o, gr, a2, gu, gel, gz, fin, gp, out_ref,
+                flat, buf, sem):
+    total = flat.shape[1]
+    cols = [(n, slice(128 * n, 128 * n + 128)) for n in range(D // 128)]
+    for n, col in cols:
+        flat[n, pl.ds(0, 16), :] = small[:, col]
+    start = 16
+    for lhs, rhs, ways in ((px, ge, 1), (a, gq, 3), (o, gr, 1), (a2, gu, 4), (gel, gz, 1), (fin, gp, 1)):
+        depth = lhs.shape[1]
+
+        def tile(i, c, lhs=lhs, rhs=rhs, ways=ways, start=start):
+            left = lhs[:, pl.ds(pl.multiple_of(i * 256, 256), 256)]
+            for w in range(ways):
+                part = lax.dot_general(left, rhs[:, w * D : (w + 1) * D], LHS_T,
+                                       preferred_element_type=jnp.float32)
+                for n, col in cols:
+                    if ways == 1:
+                        flat[n, pl.ds(pl.multiple_of(start + i * 256, 8), 256), :] = part[:, col]
+                    else:
+                        first = start + i * 256 * ways + w
+                        flat[n, pl.ds(first, 256, stride=ways), :] = part[:, col]
+            return c
+
+        lax.fori_loop(0, depth // 256, tile, 0)
+        start += depth * ways
+    for n, col in cols:
+        flat[n, pl.ds(start, total - start), :] = jnp.zeros((total - start, 128), jnp.float32)
+    owners, tiles = out_ref.shape[0], out_ref.shape[1]
+
+    def put(n, slot):
+        return pltpu.make_async_copy(buf.at[slot], out_ref.at[n], sem.at[slot])
+
+    def owner(n, c):
+        slot = n % 2
+
+        @pl.when(n >= 2)
+        def _():
+            put(n - 2, slot).wait()
+
+        def pair(t, c):
+            for h in range(2):
+                j = order_ref[(n * tiles + t) * 2 + h]
+                for m, col in cols:
+                    buf[slot, t, 4 * h : 4 * h + 4, col] = flat[m, pl.ds(4 * j, 4), :]
+            return c
+
+        lax.fori_loop(0, tiles, pair, 0)
+        put(n, slot).start()
+        return c
+
+    lax.fori_loop(0, owners, owner, 0)
+    put(owners - 2, (owners - 2) % 2).wait()
+    put(owners - 1, (owners - 1) % 2).wait()
+
+
+def packed_grads(order, small, pairs, dp):
+    blocks = order.shape[0]
+    tiles = blocks * CR // 8 // dp
+    ops = [m for pair in pairs for m in pair]
+    return pl.pallas_call(
+        grad_kernel,
+        out_shape=jax.ShapeDtypeStruct((dp, tiles, 8, D), jnp.float32),
+        in_specs=[pl.BlockSpec(memory_space=pltpu.SMEM)]
+        + [pl.BlockSpec(memory_space=pltpu.VMEM)] * (1 + len(ops)),
+        out_specs=pl.BlockSpec(memory_space=pl.ANY),
+        scratch_shapes=[
+            pltpu.VMEM((D // 128, blocks * CR, 128), jnp.float32),
+            pltpu.VMEM((2, tiles, 8, D), jnp.float32),
+            pltpu.SemaphoreType.DMA((2,)),
+        ],
+        compiler_params=pltpu.CompilerParams(vmem_limit_bytes=67043328),
+        name="pack_grads",
+    )(order, small, *ops)
 
 
 def slot_info(split_rows, seq_side):
@@ -579,12 +682,6 @@
 
 def matmul_f32(left_mat, right_mat):
     return jnp.dot(left_mat, right_mat, preferred_element_type=jnp.float32)
-
-
-def weight_grad(left_mat, right_mat):
-    return lax.dot_general(
-        left_mat, right_mat, (((0,), (0,)), ((), ())), preferred_element_type=jnp.float32
-    )
 
 
 def back_dot(left_mat, right_mat):
@@ -703,18 +800,18 @@
     length = queries.shape[1]
     blocks = [(keys_loc, values_loc, key_live)] + far_blocks
     grad_branch = grad_out.astype(jnp.bfloat16)
-    gradients["w_two"] = weight_grad(gelled, grad_branch)
+    gradients["w_two"] = (gelled, grad_branch)
     gradients["b_two"] = column_sums(grad_branch)
     unused, gelu_pull = jax.vjp(jax.nn.gelu, upward)
     grad_up = gelu_pull(back_dot(grad_branch, params["w_two"]))[0].astype(jnp.bfloat16)
-    gradients["w_one"] = weight_grad(normed_two_in, grad_up)
+    gradients["w_one"] = (normed_two_in, grad_up)
     gradients["b_one"] = column_sums(grad_up)
     grad_two, gradients["ln2_g"], gradients["ln2_b"] = norm_back(
         back_dot(grad_up, params["w_one"]), normed_two, inverse_two, vector(params, "ln2_g")
     )
     grad_hidden = grad_out + grad_two
     grad_attn = grad_hidden.astype(jnp.bfloat16)
-    gradients["w_out"] = weight_grad(mixed_out, grad_attn)
+    gradients["w_out"] = (mixed_out, grad_attn)
     gradients["b_out"] = column_sums(grad_attn)
     grad_mixed = (
         back_dot(grad_attn, params["w_out"]).astype(jnp.bfloat16).reshape(-1, length, HEADS, HD)
@@ -761,7 +858,7 @@
     grad_packed = (
         jnp.stack([grad_queries, grad_keys, grad_values], 2).astype(jnp.bfloat16).reshape(-1, 3 * D)
     )
-    gradients["w_qkv"] = weight_grad(normed_in, grad_packed)
+    gradients["w_qkv"] = (normed_in, grad_packed)
     grad_first, gradients["ln1_g"], gradients["ln1_b"] = norm_back(
         back_dot(grad_packed, params["w_qkv"]), normed, inverse, vector(params, "ln1_g")
     )
@@ -802,8 +899,8 @@
         )
         masked_count = lax.psum(chip_count, "dp")
     inverse_order = jnp.argsort(span_order)
-    params = unpack(gathered[inverse_order].reshape(-1, D))
-    teacher_params = unpack(teacher_all[inverse_order].reshape(-1, D))
+    params = sorted_weights(gathered, inverse_order)
+    teacher_params = sorted_weights(teacher_all, inverse_order)
     seq_side = lax.axis_index("seq")
     is_patch, is_cls, grid_cell = slot_info(split_rows, seq_side)
     far_patch, far_cls, far_cell = slot_info(split_rows, 1 - seq_side)
@@ -857,7 +954,7 @@
         jnp.where(selected, jnp.clip(difference / BETA, -1.0, 1.0), 0.0) * loss_scale
     ).astype(jnp.bfloat16)
     gradients = {}
-    gradients["w_head"] = weight_grad(final_in, grad_pred)
+    gradients["w_head"] = (final_in, grad_pred)
     gradients["b_head"] = column_sums(grad_pred)
     grad_tokens, gradients["lnf_g"], gradients["lnf_b"] = norm_back(
         back_dot(grad_pred, params["w_head"]), final_normed, final_inverse, vector(params, "lnf_g")
@@ -867,19 +964,25 @@
     grad_slots = grad_tokens.reshape(images, length, D)
     visible = (is_patch & jnp.logical_not(hidden_mask))[..., None]
     grad_embed = jnp.where(visible, grad_slots, 0.0).astype(jnp.bfloat16).reshape(-1, D)
-    gradients["w_pe"] = weight_grad(pixels, grad_embed)
+    gradients["w_pe"] = (pixels, grad_embed)
     gradients["b_pe"] = column_sums(grad_embed)
     gradients["mask_tok"] = jnp.sum(jnp.where(hidden_mask[..., None], grad_slots, 0.0), (0, 1))
     gradients["cls"] = jnp.sum(jnp.where(is_cls[..., None], grad_slots, 0.0), (0, 1))
-    stored_grad = reorder(pack_flat(gradients, span_order.shape[0] * CR), span_order)
+    small = jnp.concatenate(
+        [jnp.stack([gradients[name] for name in VECTORS]), gradients["b_one"].reshape(-1, D)], 0
+    )
+    stored_grad = packed_grads(
+        span_order, small, [gradients[name] for name, rows, ways in NARROW[1:]], dp
+    )
     if own_kernels:
         owned_grad, totals = scatter_all(
-            stored_grad.reshape(dp, -1, 8, D), jnp.broadcast_to(part_loss, (8, 128)), 2
+            stored_grad, jnp.broadcast_to(part_loss, (8, 128)), 2
         )
         owned_grad = owned_grad.reshape(-1, D)
         total_loss, squares = (totals[0, 0], totals[1, 0])
     else:
-        owned_grad = lax.psum_scatter(stored_grad, "dp", scatter_dimension=0, tiled=True)
+        owned_grad = lax.psum_scatter(
+            stored_grad.reshape(-1, D), "dp", scatter_dimension=0, tiled=True)
         owned_grad = lax.psum(owned_grad, "seq")
         total_loss = lax.psum(part_loss, ("dp", "seq"))
         squares = lax.psum(jnp.sum(owned_grad * owned_grad), "dp")

time: 962 us -> 636 us (0.66)
  local copies, waits for them, and re-layouts: 423 us -> 43 us
  Pallas kernels: 403 us -> 486 us
  matrix products: 78.7 us -> 49.8 us
    reshape x20 -> x2, local copies, waits for them, and re-layouts: 130 us -> 3.3 us  [the longest x1 1.99 us: attend(): return (mixed_out.astype(jnp.bfloat16).reshape(-1, D), logsum)]
    gather x3 -> x0, local copies, waits for them, and re-layouts: 85.1 us -> none  [the longest x1 32.5 us: reorder(): return stored.reshape(order.shape[0], -1, D)[order].reshape(-1, D)]
    pallas_call x0 -> x3, Pallas kernels: none -> 82.8 us  [the longest x2 47.3 us: sorted_weights(): pl.pallas_call(sort_kernel, out_shape=[jax.ShapeDtypeStruct(s, bf) for s...]
    concatenate x1, local copies, waits for them, and re-layouts: 78.5 us -> 1.28 us  [on_device(): jnp.concatenate([jnp.stack([gradients[name] for name in VECTORS]), gradie...]
    slice x16 -> x0, local copies, waits for them, and re-layouts: 54.9 us -> none  [the longest x15 53.3 us: unpack(): tables[entry_name] = flat[offset:offset + entry_rows].reshape(entry_shape)]
    another operation x1 -> x13, local copies, waits for them, and re-layouts: 38.5 us -> 10.8 us  [the longest x12 9.56 us: on_device(): jnp.stack([gradients[name] for name in VECTORS])]
    dot_general x6 -> x0, matrix products: 23.2 us -> none  [weight_grad(): lax.dot_general(left_mat, right_mat, (((0,), (0,)), ((), ())), preferred_...]
    unnamed x210 -> x170, local copies, waits for them, and re-layouts: 18.9 us -> 8.03 us
  transfers between devices with their start and end apart: 2 -> 2, of which waited for: 0 -> 0; matrix products, arithmetic and copies ran while one was open for 10% -> 4% of each run, Pallas kernels for 0% -> 0%
where the time goes in v2:
time: 636 us; the launch traced here: 630 us
  Pallas kernels  486 us (76%)
  matrix products  49.8 us (8%)
  other arithmetic  44.4 us (7%)
  local copies, waits for them, and re-layouts  43 us (7%)
    pallas_call x1, Pallas kernels, scatter_all(): pl.pallas_call(functools.partial(scatter_kernel, cuts), out_shape=[jax.Sh...  216 us
    pallas_call x1, Pallas kernels, gather_all(): pl.pallas_call(functools.partial(gather_kernel, nq, nk), out_shape=shapes...  187 us
    pallas_call x2, Pallas kernels, sorted_weights(): pl.pallas_call(sort_kernel, out_shape=[jax.ShapeDtypeStruct(s, bf) for s...  47.3 us
    pallas_call x1, Pallas kernels, packed_grads(): pl.pallas_call(grad_kernel, out_shape=jax.ShapeDtypeStruct((dp, tiles, 8,...  35.4 us
    dot_general x10, matrix products, matmul_f32(): return jnp.dot(left_mat, right_mat, preferred_element_type=jnp.float32)  22 us
  transfers between devices with their start and end apart: 2, of which 0 were waited for; matrix products, arithmetic and copies ran while one was open for 4% of the time, Pallas kernels for 0%

profile of v2, /device:TPU:0, one launch (start us, length us, event | category | flops | bytes accessed | tf_op | source)
XLA Modules:
  0.0 629.9 jit_solution(16073313288451847823)
XLA Ops:
  5.4 1.3 fusion.100
  6.6 3.2 gather_fusion
  12.3 5.8 sort.17
  19.4 187.2 %gather_all.1 = (bf16[16,170,4,768]{3,2,1,0:T(4,128)(2,1)}, bf16[16,170,4,768]{3,2,1,0:T(4,128)(2,1)}, f32[16,4,8,128]{3,2,1,0:T(8,128)}) custom-call(bf16[170,4,768]{2,1,0:T(4,128)(2,1)} %reshape.878.refs_0_, bf16[170,4,768]{2,1,0:T(4,128)(2,1)} %reshape.879.refs_1_, f32[4,8,128]{2,1,0:T(8,128)} %broadcast_in_dim.196.refs_2_), custom_call_target="tpu_custom_call" | custom-call | tf_op jit(solution)/shard_map/gather_all/pallas_call | solution.py:217
  206.5 23.8 %sort_weights.2 = (bf16[1,16,768]{2,1,0:T(8,128)(2,1)}, bf16[48,16,768]{2,1,0:T(8,128)(2,1)}, bf16[768,2304]{1,0:T(8,128)(2,1)}, bf16[48,16,768]{2,1,0:T(8,128)(...) custom-call(s32[2720]{0:T(1024)} %get-tuple-element.25.inv_ref, ...), custom_call_target="tpu_custom_call" | custom-call | tf_op jit(solution)/shard_map/sort_weights/pallas_call | solution.py:558
  230.4 23.5 %sort_weights.3 = (bf16[1,16,768]{2,1,0:T(8,128)(2,1)}, bf16[48,16,768]{2,1,0:T(8,128)(2,1)}, bf16[768,2304]{1,0:T(8,128)(2,1)}, bf16[48,16,768]{2,1,0:T(8,128)(...) custom-call(s32[2720]{0:T(1024)} %get-tuple-element.25.inv_ref, ...), custom_call_target="tpu_custom_call" | custom-call | tf_op jit(solution)/shard_map/sort_weights/pallas_call | solution.py:558
  253.9 1.6 convert_reduce_fusion.7
  255.5 2.5 multiply_sine_fusion.1
  258.1 1.3 not_and_fusion
  259.4 2.2 fusion.130
  264.6 1.6 fusion.125
  272.7 2.0 fusion.126
  274.9 1.3 pad_maximum_fusion
  278.5 1.5 slice_reduce_fusion
  280.8 1.5 fusion.134
  282.4 2.3 fusion.129
  284.7 1.5 fusion.135
  287.7 1.5 fusion.38
  291.0 7.5 %fusion.137 = (f32[256]{0:T(256)}, f32[256,768]{1,0:T(8,128)S(1)}) fusion(f32[768]{0:T(1024)} %get-tuple-element.71, f32[256,768]{1,0:T(8,128)S(1)} %get-tuple-element.148, bf16[3072,768]{1,0:T(8,128)(2,1)} %bitcast.332, bf16[768,3072]{1,0:T(8,128)(2,1)} %get-tuple-element.39, f32[3072]{0:T(1024)S(1)} %reshape.917, f32[768]{0:T(1024)} %get-tuple-element.72, ...), kind=kOutput, calls=%fused_computation.296 | convolution fusion | flops 2425356032 | bytes 11034624 | tf_op jit(solution)/shard_map/dot_general | solution.py:684
  299.5 1.7 fusion.131
  302.2 1.5 fusion.39
  305.6 5.2 multiply_convert_fusion
  310.9 1.5 fusion.133
  314.1 1.4 convert_reduce_fusion.1
  317.6 3.7 convert_reduce_fusion
  321.4 2.2 multiply_reduce_fusion.3
  323.6 1.8 convert_reduce_fusion.3
  330.1 1.8 multiply_reduce_fusion
  331.9 1.6 multiply_convert_fusion.2
  337.0 2.0 copy.65.o
  339.7 1.3 stack.86
  342.2 1.3 reshape.895
  343.5 1.3 stack.81
  344.8 1.3 stack.83
  346.1 1.3 stack.80
  347.3 1.3 stack.82
  348.6 1.3 stack.85
  349.8 1.3 fusion.64
  351.2 1.3 fusion.40
  352.5 1.3 convert_element_type.420
  357.7 1.9 multiply_reduce_fusion.4
  359.8 1.5 copy.64.gq
  363.4 1.7 convert_reduce_fusion.4
  365.5 1.3 concatenate.9.small
  366.7 35.4 %pack_grads.1 = f32[16,85,8,768]{3,2,1,0:T(8,128)} custom-call(s32[2720]{0:T(1024)} %order_ref.1, f32[16,768]{1,0:T(8,128)} %concatenate.9.small, bf16[256,768]{1,0:T(8,128)(2,1)} %bitcast.324, bf16[256,768]{1,0:T(8,128)(2,1)} %get-tuple-element.99.ge, bf16[256,768]{1,0:T(8,128)(2,1)} %copy-done.21, bf16[256,2304]{1,0:T(8,128)(2,1)} %copy.64.gq, ...), custom_call_target="tpu_custom_call" | custom-call | tf_op jit(solution)/shard_map/pack_grads/pallas_call | solution.py:638
  402.8 216.2 %scatter_all.1 = (f32[85,8,768]{2,1,0:T(8,128)}, f32[8,128]{1,0:T(8,128)}) custom-call(f32[4,2,2,85,8,768]{5,4,3,2,1,0:T(8,128)} %bitcast.306, f32[8,128]{1,0:T(8,128)} %broadcast_in_dim.209.note_ref), custom_call_target="tpu_custom_call" | custom-call | tf_op jit(solution)/shard_map/scatter_all/pallas_call | solution.py:477
  619.0 1.3 fusion.127
  621.0 7.5 %fusion.120 = (bf16[680,768]{1,0:T(8,128)(2,1)}, f32[680,768]{1,0:T(8,128)}, f32[680,768]{1,0:T(8,128)}, f32[680,768]{1,0:T(8,128)}) fusion(f32[680,768]{1,0:T(8,128)} %param.13, f32[]{:T(128)} %bitcast.54, f32[]{:T(128)} %bitcast.53, f32[85,8,768]{2,1,0:T(8,128)} %get-tuple-element.43, f32[]{:T(128)S(6)} %div.124, f32[680,768]{1,0:T(8,128)} %param.16, ...), kind=kLoop, calls=%fused_computation.283 | loop fusion | flops 8878080 | bytes 15667212 | tf_op jit(solution)/shard_map/convert_element_type | solution.py:1004
  (263 shorter events, 46.4 us)
Async XLA Ops:
  0.6 9.2 %copy-start.30 = (bf16[680,768]{1,0:T(8,128)(2,1)S(1)}, bf16[680,768]{1,0:T(8,128)(2,1)}, u32[]{:S(2)}) copy-start(bf16[680,768]{1,0:T(8,128)(2,1)} %param.14) | copy-start | bytes 3133444
  6.6 4.4 copy-start.3
  259.4 7.6 %copy-start.64 = (pred[256]{0:T(512)(128)(4,1)}, pred[256]{0:T(512)(128)(4,1)S(1)}, u32[]{:S(2)}) copy-start(pred[256]{0:T(512)(128)(4,1)S(1)} %get-tuple-element.102) | copy-start | bytes 772
  259.4 7.6 %copy-start.66 = (pred[256]{0:T(512)(128)(4,1)}, pred[256]{0:T(512)(128)(4,1)S(1)}, u32[]{:S(2)}) copy-start(pred[256]{0:T(512)(128)(4,1)S(1)} %get-tuple-element.155) | copy-start | bytes 772
  259.4 3.0 copy-start.75
  264.6 2.5 copy-start.33
  264.6 2.5 copy-start.77
  267.8 2.4 copy-start.73
  268.0 3.3 copy-start.57
  274.7 7.7 %copy-start.13 = (bf16[2,128,1,12,64]{1,0,4,3,2:T(2,128)(2,1)}, bf16[2,128,1,12,64]{1,0,4,3,2:T(2,128)(2,1)S(1)}, u32[]{:S(2)}) copy-start(bf16[2,128,1,12,64]{1,0,4,3,2:T(2,128)(2,1)S(1)} %get-tuple-element.109) | copy-start | bytes 1179652
  274.7 27.1 %copy-start.7 = (bf16[2,128,1,12,64]{1,0,4,3,2:T(2,128)(2,1)}, bf16[2,128,1,12,64]{1,0,4,3,2:T(2,128)(2,1)S(1)}, u32[]{:S(2)}) copy-start(bf16[2,128,1,12,64]{1,0,4,3,2:T(2,128)(2,1)S(1)} %get-tuple-element.108) | copy-start | bytes 1179652
  274.9 5.8 copy-start.59
  274.9 5.8 copy-start.60
  274.9 5.8 copy-start.68
  274.9 5.8 copy-start.69
  274.9 5.8 copy-start.70
  274.9 5.9 copy-start.28
  276.3 8.4 %collective-permute-start = (bf16[4,2,128,12,64]{2,4,3,1,0:T(8,128)(2,1)}, bf16[4,2,128,12,64]{2,4,3,1,0:T(8,128)(2,1)}, u32[]{:S(2)}, u32[]{:S(2)}) collective-permute-start(bf16[4,2,128,12,64]{2,4,3,1,0:T(8,128)(2,1)} %pad_maximum_fusion), channel_id=1, source_target_pairs={{0,1},{1,0},{2,3},{3,2},{4,5},{5,4},{6,7},{7,6},{8,9},{9,8},{10,11... | collective-permute-start | bytes 4718600 | tf_op jit(solution)/shard_map/ppermute | solution.py:32
  280.8 3.9 copy-start.71
  282.4 2.3 copy-start.35
  287.6 2.0 copy-start.29
  304.9 6.0 slice-start.2
  305.4 5.5 copy-start.22
  305.6 5.3 copy-start.63
  305.6 5.3 slice-start.3
  313.0 2.5 copy-start.23
  316.7 4.6 slice-start
  317.6 3.7 copy-start.24
  317.6 3.7 slice-start.1
  321.3 2.2 copy-start.26
  333.5 2.7 copy-start.17
  334.2 15.7 %copy-start.6 = (bf16[2,12,128,128]{2,3,1,0:T(8,128)(2,1)S(1)}, bf16[2,12,128,128]{2,3,1,0:T(8,128)(2,1)}, u32[]{:S(2)}) copy-start(bf16[2,12,128,128]{2,3,1,0:T(8,128)(2,1)} %get-tuple-element.111) | copy-start | bytes 2359300
  335.1 17.4 %collective-permute-start.1 = (bf16[2,2,128,12,64]{2,4,3,1,0:T(8,128)(2,1)}, bf16[2,2,128,12,64]{2,4,3,1,0:T(8,128)(2,1)}, u32[]{:S(2)}, u32[]{:S(2)}) collective-permute-start(bf16[2,2,128,12,64]{2,4,3,1,0:T(8,128)(2,1)} %pad_maximum_fusion.3), channel_id=1, source_target_pairs={{0,1},{1,0},{2,3},{3,2},{4,5},{5,4},{6,7},{7,6},{8,9},{9,8},{10,11... | collective-permute-start | bytes 2359304 | tf_op jit(solution)/shard_map/ppermute | solution.py:32
  337.0 14.2 %copy-start.5 = (bf16[2,12,128,128]{2,3,1,0:T(8,128)(2,1)S(1)}, bf16[2,12,128,128]{2,3,1,0:T(8,128)(2,1)}, u32[]{:S(2)}) copy-start(bf16[2,12,128,128]{2,3,1,0:T(8,128)(2,1)} %copy-done.4) | copy-start | bytes 2359300
  355.5 2.0 copy-start.74
  355.7 2.1 copy-start.2
  355.7 2.1 copy-start.40
  355.7 2.1 copy-start.44
  355.7 2.1 copy-start.58
  359.8 3.5 copy-start.20
  363.3 2.0 copy-start.38
  363.3 2.0 copy-start.49
  363.4 2.0 copy-start.50
  363.4 2.0 copy-start.51
  363.4 2.0 copy-start.52
  363.4 2.0 copy-start.53
  363.4 2.0 copy-start.54
  363.4 2.0 copy-start.55
  (36 other events, 48.1 us)
